TPU v7x, 32 devices: a whole 2x2x4 slice. The times are simulated.
32 devices in a mesh: dp: 4 (over z), seq: 8 (over y, x, core).
Axes of the slice: x: 2, y: 2, z: 4, core: 2. Of those that a mesh axis runs over, the one named last changes fastest.
Arguments:
- tokens: bfloat16 [4, 4096, 768], P('dp', 'seq'), may hold values from -6 to 6
- cotangent: bfloat16 [4, 4096, 768], P('dp', 'seq'), may hold values from -6 to 6
- norm_gain: bfloat16 [768], P(('dp', 'seq')), may hold values from 0.5 to 1.5
- in_weight: bfloat16 [768, 3352], P(('dp', 'seq')), may hold values from -2 to 2
- conv_weight: bfloat16 [4, 1792], P(None, ('dp', 'seq')), may hold values from -3 to 3
- conv_bias: bfloat16 [1792], P(('dp', 'seq')), may hold values from -3 to 3
- dt_bias: float32 [24], replicated, may hold values from -8 to -6
- a_log: float32 [24], replicated, may hold values from -10 to 0
- d_skip: float32 [24], replicated, may hold values from 0.5 to 2
- gate_gain: bfloat16 [1536], P(('dp', 'seq')), may hold values from 0.5 to 1.5
- out_weight: bfloat16 [1536, 768], P(('dp', 'seq')), may hold values from -0.15625 to 0.15625
Outputs:
- block_out: bfloat16 [4, 4096, 768], P('dp', 'seq')
- input_grad: bfloat16 [4, 4096, 768], P('dp', 'seq')
- norm_grad: float32 [768], P(('dp', 'seq'))
- inward_grad: float32 [768, 3352], P(('dp', 'seq'))
- kernel_grad: float32 [4, 1792], P(None, ('dp', 'seq'))
- offset_grad: float32 [1792], P(('dp', 'seq'))
- step_grad: float32 [24], replicated
- decay_grad: float32 [24], replicated
- skip_grad: float32 [24], replicated
- gain_grad: float32 [1536], P(('dp', 'seq'))
- outward_grad: float32 [1536, 768], P(('dp', 'seq'))
All inputs are finite; a program needn't handle non-finite values.
Results may differ from a plain program's by a relative error of at most 0.018.
Values may be sent and summed in bfloat16 or wider, within the bound.
A program may use at most 256 MiB of HBM per device.

v0:
```python
import functools

import jax
import jax.numpy as jnp
from jax import lax
from jax.experimental import pallas as pl
from jax.experimental.pallas import tpu as pltpu
from jax.sharding import PartitionSpec as P

MESH = pl.DeviceIdType.MESH
NHEADS = 24
HEADDIM = 64
NSTATE = 128
KCONV = 4
DI = 1536
DC = 1792
Q = 128
LANES = 128
PAIRS = DI // LANES
HALF = DI // 2
epsilon = 1e-05
highest = lax.Precision.HIGHEST
f32 = jnp.float32
bf16 = jnp.bfloat16


def mm(a, b):
    return lax.dot_general(a, b, (((1,), (0,)), ((), ())), preferred_element_type=f32)


def mm_nt(a, b):
    return lax.dot_general(a, b, (((1,), (1,)), ((), ())), preferred_element_type=f32)


def mm_exact(a, b):
    return lax.dot_general(
        a, b, (((1,), (0,)), ((), ())), precision=highest, preferred_element_type=f32
    )


def sigmoid(v):
    return 1.0 / (1.0 + jnp.exp(-v))


def fold_rows(v):
    return jnp.sum(v.reshape(v.shape[0] // 8, 8, v.shape[1]), axis=0)


def ssd_kernel(
    seq_size,
    proj,
    grad_low,
    taps,
    cbias,
    heads,
    gain,
    gate_low,
    grad_proj,
    sum_conv,
    sum_gate,
    sum_head,
    cpad,
    act,
    dsilu,
    gpad,
    yint,
    yst,
    ws,
    sg,
    gs,
    ex_e,
    ex_f,
    ex_dt,
    cum,
    cum_t,
    dts,
    logd,
    sgm,
    grad_a,
    states,
    adjs,
    s0,
    g0,
    conv_edge,
    grad_edge,
    full_send,
    full_recv,
    half_send,
    half_recv,
    swap_send,
    swap_recv,
    log_send,
    log_recv,
    edge_sems,
    full_sems,
    half_sems,
    swap_sems,
    log_sems,
    swap_hold,
    passed,
):
    length = proj.shape[0]
    chunks = length // Q
    me = lax.axis_index("seq")
    bits = seq_size.bit_length() - 1
    bit = [(me // (1 << r)) % 2 for r in range(bits)]
    partner = [me + (1 - 2 * bit[r]) * (1 << r) for r in range(bits)]
    side = bit[0]

    barrier = pltpu.get_barrier_semaphore()
    for other in partner:
        pl.semaphore_signal(barrier, inc=1, device_id={"seq": other}, device_id_type=MESH)

    @pl.when(me > 0)
    def _():
        pl.semaphore_signal(barrier, inc=1, device_id={"seq": me - 1}, device_id_type=MESH)

    @pl.when(me < seq_size - 1)
    def _():
        pl.semaphore_signal(barrier, inc=1, device_id={"seq": me + 1}, device_id_type=MESH)

    pl.semaphore_wait(barrier, bits + jnp.where(me > 0, 1, 0) + jnp.where(me < seq_size - 1, 1, 0))

    def edge_copy():
        return pltpu.make_async_remote_copy(
            src_ref=proj.at[pl.ds(length - 16, 16), pl.ds(DI, DC)],
            dst_ref=conv_edge,
            send_sem=edge_sems.at[0],
            recv_sem=edge_sems.at[1],
            device_id={"seq": me + 1},
            device_id_type=MESH,
        )

    def grad_edge_copy():
        return pltpu.make_async_remote_copy(
            src_ref=gpad.at[pl.ds(0, 8), :],
            dst_ref=grad_edge,
            send_sem=edge_sems.at[2],
            recv_sem=edge_sems.at[3],
            device_id={"seq": me - 1},
            device_id_type=MESH,
        )

    def exchange(src, dst, sems, index, other):
        return pltpu.make_async_remote_copy(
            src_ref=src,
            dst_ref=dst,
            send_sem=sems.at[index, 0],
            recv_sem=sems.at[index, 1],
            device_id={"seq": other},
            device_id_type=MESH,
        )

    @pl.when(me < seq_size - 1)
    def _():
        edge_copy().start()

    lane_head = lax.broadcasted_iota(jnp.int32, (NHEADS, DI), 1) // HEADDIM
    spread_m = (lane_head == lax.broadcasted_iota(jnp.int32, (NHEADS, DI), 0)).astype(bf16)
    rows_i = lax.broadcasted_iota(jnp.int32, (Q, Q), 0)
    cols_i = lax.broadcasted_iota(jnp.int32, (Q, Q), 1)
    lower = (rows_i >= cols_i)
    lower_f = lower.astype(f32)
    upper_f = (rows_i <= cols_i).astype(f32)
    strict_upper = rows_i < cols_i
    low_lane = lax.broadcasted_iota(jnp.int32, (Q, LANES), 1) < HEADDIM

    def gather_m(p):
        lane = lax.broadcasted_iota(jnp.int32, (LANES, NHEADS), 0) // HEADDIM + 2 * p
        return (lane == lax.broadcasted_iota(jnp.int32, (LANES, NHEADS), 1)).astype(bf16)

    def pair(p):
        return pl.ds(p * LANES, LANES)

    def blockdiag(v):
        zero = jnp.zeros_like(v)
        return jnp.concatenate([jnp.where(low_lane, v, zero), jnp.where(low_lane, zero, v)], axis=0)

    def spread_row(row):
        hi = row.astype(bf16)
        rest = row - hi.astype(f32)
        mid = rest.astype(bf16)
        lo = (rest - mid.astype(f32)).astype(bf16)
        return mm(hi, spread_m) + mm(mid, spread_m) + mm(lo, spread_m)

    dt_bias = heads[0:1, :]
    rate = jnp.exp(heads[1:2, :])
    skip_wide = spread_row(jnp.broadcast_to(heads[2:3, :], (8, NHEADS)))[0:1, :]

    def rates(c, carry):
        rows = pl.ds(pl.multiple_of(c * Q, Q), Q)
        raw = proj[rows, pl.ds(DI + DC, NHEADS)].astype(f32) + dt_bias
        dt = jnp.maximum(raw, 0.0) + jnp.log1p(jnp.exp(-jnp.abs(raw)))
        ld = -dt * rate
        run = mm_exact(lower_f, ld)
        dts[rows, :] = dt
        logd[rows, :] = ld
        sgm[rows, :] = sigmoid(raw)
        cum[rows, :] = run
        wide = jnp.concatenate([run, jnp.zeros((Q, LANES - NHEADS), f32)], axis=1)
        cum_t[c] = wide.T[0:NHEADS, :]
        last = run[Q - 1 : Q, :]
        ex_e[rows, :] = mm(jnp.exp(run).astype(bf16), spread_m).astype(bf16)
        ex_f[rows, :] = mm(jnp.exp(last - run).astype(bf16), spread_m).astype(bf16)
        ex_dt[rows, :] = mm(dt.astype(bf16), spread_m).astype(bf16)
        return carry + last

    log_total = lax.fori_loop(0, chunks, rates, jnp.zeros((1, NHEADS), f32))

    def load_conv(c, carry):
        rows = pl.ds(pl.multiple_of(c * Q, Q), Q)
        cpad[pl.ds(pl.multiple_of(c * Q + 8, 8), Q), :] = proj[rows, pl.ds(DI, DC)].astype(f32)
        return carry

    lax.fori_loop(0, chunks, load_conv, 0)

    @pl.when(me > 0)
    def _():
        edge_copy().wait_recv()
        cpad[0:8, :] = conv_edge[...].astype(f32)[8:16, :]

    @pl.when(me == 0)
    def _():
        cpad[0:8, :] = jnp.zeros((8, DC), f32)

    @pl.when(me < seq_size - 1)
    def _():
        edge_copy().wait_send()

    def conv_block(c, block):
        lanes = pl.ds(block * LANES, LANES)
        window = cpad[pl.ds(pl.multiple_of(c * Q, Q), Q + 8), lanes]
        pre = cbias[0:1, lanes] + sum(
            taps[k : k + 1, lanes] * window[5 + k : 5 + k + Q, :] for k in range(KCONV)
        )
        gate = sigmoid(pre)
        value = pre * gate
        rows = pl.ds(pl.multiple_of(c * Q, Q), Q)
        act[rows, lanes] = value
        dsilu[rows, lanes] = gate + value * (1.0 - gate)

    def local_states(c, carry):
        rows = pl.ds(pl.multiple_of(c * Q, Q), Q)
        for block in range(DC // LANES):
            conv_block(c, block)
        decay = spread_row(jnp.exp(jnp.broadcast_to(cum_t[c][:, Q - 1 : Q], (NHEADS, 8)).T))[0:1, :]
        in_t = act[rows, pl.ds(DI, NSTATE)].T.astype(bf16)
        for p in range(PAIRS):
            xw = act[rows, pair(p)] * (ex_f[rows, pair(p)].astype(f32) * ex_dt[rows, pair(p)].astype(f32))
            states[c + 1, :, pair(p)] = decay[:, p * LANES : (p + 1) * LANES] * states[
                c, :, pair(p)
            ] + mm(in_t, xw.astype(bf16))
        return carry

    states[0] = jnp.zeros((NSTATE, DI), f32)
    lax.fori_loop(0, chunks, local_states, 0)

    log_send[0] = jnp.concatenate(
        [jnp.broadcast_to(log_total, (8, NHEADS)), jnp.zeros((8, LANES - NHEADS), f32)], axis=1
    )


    side_f = side.astype(f32)
    half_lane = (lax.broadcasted_iota(jnp.int32, (NHEADS, HALF), 1) + side * HALF) // HEADDIM
    spread_half = (half_lane == lax.broadcasted_iota(jnp.int32, (NHEADS, HALF), 0)).astype(bf16)

    def widen(row, matrix):
        hi = row.astype(bf16)
        rest = row - hi.astype(f32)
        mid = rest.astype(bf16)
        return (mm(hi, matrix) + mm(mid, matrix))[0:1, :]

    def scan_ops(way, total, out):
        near = [(bit[r] if way == 0 else 1 - bit[r]).astype(f32) for r in range(bits)]

        def full():
            return exchange(full_send.at[way], full_recv.at[way], full_sems, way, partner[0])

        def half(r):
            k = way * bits + r
            return exchange(half_send.at[k], half_recv.at[k], half_sems, k, partner[r])

        def swap():
            return exchange(swap_send.at[way], swap_recv.at[way], swap_sems, way, partner[0])

        def logs(r):
            return exchange(log_send.at[r], log_recv.at[r], log_sems, r, partner[r])

        def start():
            for s in range(2):
                full_send[way, s] = total[:, s * HALF : (s + 1) * HALF].astype(bf16)
            full().start()
            if way == 0:
                logs(0).start()
            passed[way] = jnp.zeros((8, NHEADS), f32)

        def step(r):
            if r == 0:
                full().wait()
            else:
                half(r).wait()
            if way == 0:
                logs(r).wait()
                if r + 1 < bits:
                    log_send[r + 1] = log_send[r] + log_recv[r]
            log_mine = log_send[r][:, 0:NHEADS]
            log_theirs = log_recv[r][:, 0:NHEADS]
            if r == 0:
                mine = full_send[way, side].astype(f32)
                theirs = full_recv[way, side].astype(f32)
                held = jnp.zeros((NSTATE, HALF), f32)
            else:
                mine = half_send[way * bits + r].astype(f32)
                theirs = half_recv[way * bits + r].astype(f32)
                factor = near[r] * widen(jnp.exp(passed[way]), spread_half)
                held = swap_hold[way] + factor * theirs
                passed[way] = passed[way] + near[r] * log_theirs
            if r + 1 < bits:
                keep = widen(jnp.exp((1.0 - near[r]) * log_theirs), spread_half)
                take = widen(jnp.exp(near[r] * log_mine), spread_half)
                half_send[way * bits + r + 1] = (keep * mine + take * theirs).astype(bf16)
                half(r + 1).start()
                if way == 0:
                    logs(r + 1).start()
                swap_hold[way] = held
            else:
                swap_send[way] = held.astype(bf16)
                swap().start()

        def finish():
            swap().wait()
            decay = widen(jnp.exp(near[0] * log_recv[0][:, 0:NHEADS]), spread_m)
            for s in range(2):
                own = side_f if s == 1 else 1.0 - side_f
                part = own * swap_send[way].astype(f32) + (1.0 - own) * swap_recv[way].astype(f32)
                out[:, s * HALF : (s + 1) * HALF] = (
                    near[0] * full_recv[way, s].astype(f32)
                    + decay[:, s * HALF : (s + 1) * HALF] * part
                )

        def after(c):
            for r in range(min(bits, chunks)):
                pl.when(c == r)(functools.partial(step, r))

        def rest():
            for r in range(min(bits, chunks), bits):
                step(r)
            finish()

        return start, after, rest

    start, after, rest = scan_ops(0, states.at[chunks], s0)
    start()

    def rows_of(c):
        return pl.ds(pl.multiple_of(c * Q, Q), Q)

    def intra_forward(c, carry):
        rows = rows_of(c)
        in_low = act[rows, pl.ds(DI, NSTATE)].astype(bf16)
        out_low = act[rows, pl.ds(DI + NSTATE, NSTATE)].astype(bf16)
        scores = mm_nt(out_low, in_low) * lower_f
        for p in range(PAIRS):
            parts = []
            for h in (2 * p, 2 * p + 1):
                spread = cum[rows, h : h + 1] - cum_t[c, h : h + 1, :]
                parts.append((scores * jnp.exp(jnp.minimum(spread, 0.0))).astype(bf16))
            stepped = (act[rows, pair(p)] * ex_dt[rows, pair(p)].astype(f32)).astype(bf16)
            yst[rows, pair(p)] = mm(jnp.concatenate(parts, axis=1), blockdiag(stepped))
        after(c)
        return carry

    lax.fori_loop(0, chunks, intra_forward, 0)
    rest()

    sum_conv[...] = jnp.zeros_like(sum_conv)
    sum_gate[...] = jnp.zeros_like(sum_gate)
    gain_wide = gain[0:1, :]

    def state_decay(c):
        last = jnp.broadcast_to(cum_t[c][:, Q - 1 : Q], (NHEADS, 8))
        wide = jnp.concatenate([last, jnp.zeros((LANES - NHEADS, 8), f32)], axis=0)
        return wide.T[:, 0:NHEADS]

    def gating(c, before):
        rows = rows_of(c)
        decay_before = widen(jnp.exp(before), spread_m)
        out_now = act[rows, pl.ds(DI + NSTATE, NSTATE)]
        out_low = out_now.astype(bf16)
        out_t = out_now.T.astype(bf16)
        squares = jnp.zeros((Q, LANES), f32)
        for p in range(PAIRS):
            state = states[c, :, pair(p)] + decay_before[:, p * LANES : (p + 1) * LANES] * s0[
                :, pair(p)
            ]
            states[c, :, pair(p)] = state
            reached = ex_e[rows, pair(p)].astype(f32) * mm(out_low, state.astype(bf16))
            with_skip = (
                yst[rows, pair(p)]
                + reached
                + skip_wide[:, p * LANES : (p + 1) * LANES] * act[rows, pair(p)]
            )
            z = proj[rows, pair(p)].astype(f32)
            sig = sigmoid(z)
            gated = with_skip * (z * sig)
            squares += gated * gated
            yint[:, pair(p)] = reached
            ws[:, pair(p)] = with_skip
            sg[:, pair(p)] = sig
        norm = lax.rsqrt(jnp.sum(squares, axis=1, keepdims=True) * (1.0 / DI) + epsilon)
        inner = jnp.zeros((Q, LANES), f32)
        for p in range(PAIRS):
            z = proj[rows, pair(p)].astype(f32)
            gated = ws[:, pair(p)] * (z * sg[:, pair(p)])
            gain_p = gain_wide[:, p * LANES : (p + 1) * LANES]
            gate_low[rows, pair(p)] = (gated * norm * gain_p).astype(bf16)
            inner += grad_low[rows, pair(p)] * gain_p * gated
            sum_gate[0:8, pair(p)] += fold_rows(grad_low[rows, pair(p)] * (gated * norm))
        mean = jnp.sum(inner, axis=1, keepdims=True) * (1.0 / DI)
        pull = norm * norm * norm * mean
        later = jnp.zeros((Q, NHEADS), f32)
        for p in range(PAIRS):
            z = proj[rows, pair(p)].astype(f32)
            sig = sg[:, pair(p)]
            with_skip = ws[:, pair(p)]
            gain_p = gain_wide[:, p * LANES : (p + 1) * LANES]
            gated = with_skip * (z * sig)
            grad_gated = norm * (grad_low[rows, pair(p)] * gain_p) - gated * pull
            grad = grad_gated * (z * sig)
            gs[rows, pair(p)] = grad
            grad_z = grad_gated * with_skip * (sig * (1.0 + z * (1.0 - sig)))
            grad_proj[rows, pair(p)] = grad_z.astype(bf16)
            sum_gate[8:16, pair(p)] += fold_rows(grad * act[rows, pair(p)])
            later += mm((grad * yint[:, pair(p)]).astype(bf16), gather_m(p))
            scaled = (grad * ex_e[rows, pair(p)].astype(f32)).astype(bf16)
            adjs[c, :, pair(p)] = mm(out_t, scaled)
        grad_a[rows, :] = mm_exact(upper_f, later)
        return before + state_decay(c)

    lax.fori_loop(0, chunks, gating, jnp.zeros((8, NHEADS), f32))

    adjs[chunks] = jnp.zeros((NSTATE, DI), f32)

    def local_adjoints(i, carry):
        c = chunks - 1 - i
        decay = widen(jnp.exp(state_decay(c)), spread_m)
        for p in range(PAIRS):
            adjs[c, :, pair(p)] = (
                decay[:, p * LANES : (p + 1) * LANES] * adjs[c + 1, :, pair(p)]
                + adjs[c, :, pair(p)]
            )
        return carry

    lax.fori_loop(0, chunks, local_adjoints, 0)
    start, after, rest = scan_ops(1, adjs.at[0], g0)
    start()

    def intra_backward(c, carry):
        rows = rows_of(c)
        in_low = act[rows, pl.ds(DI, NSTATE)].astype(bf16)
        out_low = act[rows, pl.ds(DI + NSTATE, NSTATE)].astype(bf16)
        scores = mm_nt(in_low, out_low) * upper_f
        grad_scores = jnp.zeros((Q, Q), f32)
        tails = upper_f.T.astype(bf16)
        found = []
        for p in range(PAIRS):
            grad = gs[rows, pair(p)].astype(bf16)
            stepped = (act[rows, pair(p)] * ex_dt[rows, pair(p)].astype(f32)).astype(bf16)
            values = mm_nt(blockdiag(stepped), grad)
            weights, crosses = [], []
            for i, h in enumerate((2 * p, 2 * p + 1)):
                spread = cum_t[c, h : h + 1, :] - cum[rows, h : h + 1]
                decays = jnp.exp(jnp.minimum(spread, 0.0))
                weights.append((scores * decays).astype(bf16))
                part = decays * values[i * Q : (i + 1) * Q, :]
                grad_scores += part
                crosses.append((part * scores).astype(bf16))
            yst[rows, pair(p)] = mm(jnp.concatenate(weights, axis=1), blockdiag(grad))
            sums = mm(jnp.concatenate(crosses, axis=0), tails)
            for i in range(2):
                picked = jnp.where(strict_upper, sums[i * Q : (i + 1) * Q, :], 0.0)
                found.append(jnp.sum(picked, axis=0, keepdims=True))
        found.append(jnp.zeros((LANES - NHEADS, Q), f32))
        grad_a[rows, :] += jnp.concatenate(found, axis=0).T[:, 0:NHEADS]
        grad_low_scores = (grad_scores * upper_f).astype(bf16)
        gpad[rows, pl.ds(DI, NSTATE)] = mm(grad_low_scores, out_low)
        gpad[rows, pl.ds(DI + NSTATE, NSTATE)] = mm((grad_scores * upper_f).T.astype(bf16), in_low)
        after(c)
        return carry

    lax.fori_loop(0, chunks, intra_backward, 0)
    rest()

    sum_head[...] = jnp.zeros_like(sum_head)

    def finish_backward(c, before):
        after_log = jnp.broadcast_to(log_total, (8, NHEADS)) - before - state_decay(c)
        decay_after = widen(jnp.exp(after_log), spread_m)
        rows = rows_of(c)
        in_low = act[rows, pl.ds(DI, NSTATE)].astype(bf16)
        grad_in = gpad[rows, pl.ds(DI, NSTATE)]
        grad_out = gpad[rows, pl.ds(DI + NSTATE, NSTATE)]
        kept = jnp.zeros((Q, NHEADS), f32)
        grad_step = jnp.zeros((Q, NHEADS), f32)
        crossing = jnp.zeros((8, NHEADS), f32)
        for p in range(PAIRS):
            adj = adjs[c + 1, :, pair(p)] + decay_after[:, p * LANES : (p + 1) * LANES] * g0[
                :, pair(p)
            ]
            adj_low = adj.astype(bf16)
            state = states[c, :, pair(p)]
            x = act[rows, pair(p)]
            dt = ex_dt[rows, pair(p)].astype(f32)
            to_end = ex_f[rows, pair(p)].astype(f32)
            grad = gs[rows, pair(p)]
            later = to_end * mm(in_low, adj_low)
            total = yst[rows, pair(p)] + later
            stepped = x * dt
            pick = gather_m(p)
            kept += mm((stepped * later).astype(bf16), pick)
            grad_step += mm((x * total).astype(bf16), pick)
            crossing += mm(fold_rows(adj * state).astype(bf16), pick)
            grad_in += mm_nt((stepped * to_end).astype(bf16), adj_low)
            scaled = (grad * ex_e[rows, pair(p)].astype(f32)).astype(bf16)
            grad_out += mm_nt(scaled, state.astype(bf16))
            grad_x = dt * total + skip_wide[:, p * LANES : (p + 1) * LANES] * grad
            gpad[rows, pair(p)] = grad_x * dsilu[rows, pair(p)]
        gpad[rows, pl.ds(DI, NSTATE)] = grad_in * dsilu[rows, pl.ds(DI, NSTATE)]
        gpad[rows, pl.ds(DI + NSTATE, NSTATE)] = grad_out * dsilu[rows, pl.ds(DI + NSTATE, NSTATE)]
        whole = jnp.exp(state_decay(c))[0:1, :] * jnp.sum(crossing, axis=0, keepdims=True)
        grad_decay = grad_a[rows, :] + mm_exact(lower_f - upper_f * lower_f, kept) + whole
        grad_raw = (grad_step - rate * grad_decay) * sgm[rows, :]
        grad_proj[rows, pl.ds(DI + DC, NHEADS)] = grad_raw.astype(bf16)
        sum_head[0:8, 0:NHEADS] += fold_rows(grad_raw)
        sum_head[8:16, 0:NHEADS] += fold_rows(grad_decay * logd[rows, :])

        @pl.when(jnp.logical_and(c == 0, me > 0))
        def _():
            grad_edge_copy().start()

        return before + state_decay(c)

    lax.fori_loop(0, chunks, finish_backward, jnp.zeros((8, NHEADS), f32))

    @pl.when(me > 0)
    def _():
        grad_edge_copy().wait_send()

    @pl.when(me < seq_size - 1)
    def _():
        grad_edge_copy().wait_recv()
        gpad[pl.ds(length, 8), :] = grad_edge[...]

    @pl.when(me == seq_size - 1)
    def _():
        gpad[pl.ds(length, 8), :] = jnp.zeros((8, DC), f32)

    def conv_backward(c, carry):
        rows = rows_of(c)
        longer = pl.ds(pl.multiple_of(c * Q, Q), Q + 8)
        for block in range(DC // LANES):
            lanes = pl.ds(block * LANES, LANES)
            grads = gpad[longer, lanes]
            inputs = cpad[longer, lanes]
            grad = grads[0:Q, :]
            grad_conv = sum(
                taps[k : k + 1, lanes] * grads[KCONV - 1 - k : KCONV - 1 - k + Q, :]
                for k in range(KCONV)
            )
            grad_proj[rows, pl.ds(DI + block * LANES, LANES)] = grad_conv.astype(bf16)
            for k in range(KCONV):
                sum_conv[8 * k : 8 * k + 8, lanes] += fold_rows(grad * inputs[5 + k : 5 + k + Q, :])
            sum_conv[8 * KCONV : 8 * KCONV + 8, lanes] += fold_rows(grad)
        return carry

    lax.fori_loop(0, chunks, conv_backward, 0)


def ssd_call(seq_size, proj, grad_low, taps, cbias, heads, gain):
    length = proj.shape[0]
    chunks = length // Q
    bits = seq_size.bit_length() - 1
    vmem = lambda shape, kind=f32: pltpu.VMEM(shape, kind)
    space = pl.BlockSpec(memory_space=pltpu.VMEM)
    return pl.pallas_call(
        functools.partial(ssd_kernel, seq_size),
        name="ssd",
        out_shape=(
            jax.ShapeDtypeStruct((length, DI), bf16),
            jax.ShapeDtypeStruct((length, proj.shape[1]), bf16),
            jax.ShapeDtypeStruct((8 * (KCONV + 1), DC), f32),
            jax.ShapeDtypeStruct((16, DI), f32),
            jax.ShapeDtypeStruct((16, LANES), f32),
        ),
        in_specs=[space] * 6,
        out_specs=[space] * 5,
        scratch_shapes=[
            vmem((length + 8, DC)),
            vmem((length, DC)),
            vmem((length, DC)),
            vmem((length + 8, DC)),
            vmem((Q, DI)),
            vmem((length, DI)),
            vmem((Q, DI)),
            vmem((Q, DI)),
            vmem((length, DI)),
            vmem((length, DI), bf16),
            vmem((length, DI), bf16),
            vmem((length, DI), bf16),
            vmem((length, NHEADS)),
            vmem((chunks, NHEADS, Q)),
            vmem((length, NHEADS)),
            vmem((length, NHEADS)),
            vmem((length, NHEADS)),
            vmem((length, NHEADS)),
            vmem((chunks + 1, NSTATE, DI)),
            vmem((chunks + 1, NSTATE, DI)),
            vmem((NSTATE, DI)),
            vmem((NSTATE, DI)),
            vmem((16, DC), bf16),
            vmem((8, DC)),
            vmem((2, 2, NSTATE, HALF), bf16),
            vmem((2, 2, NSTATE, HALF), bf16),
            vmem((2 * bits, NSTATE, HALF), bf16),
            vmem((2 * bits, NSTATE, HALF), bf16),
            vmem((2, NSTATE, HALF), bf16),
            vmem((2, NSTATE, HALF), bf16),
            vmem((bits, 8, LANES)),
            vmem((bits, 8, LANES)),
            pltpu.SemaphoreType.DMA((4,)),
            pltpu.SemaphoreType.DMA((2, 2)),
            pltpu.SemaphoreType.DMA((2 * bits, 2)),
            pltpu.SemaphoreType.DMA((2, 2)),
            pltpu.SemaphoreType.DMA((bits, 2)),
            vmem((2, NSTATE, HALF)),
            vmem((2, 8, NHEADS)),
        ],
        compiler_params=pltpu.CompilerParams(
            collective_id=1, has_side_effects=True, vmem_limit_bytes=62 * 1024 * 1024
        ),
    )(proj, grad_low, taps, cbias, heads, gain)


def rms_scale(values, weight):
    return values * lax.rsqrt(jnp.mean(values * values, axis=-1, keepdims=True) + epsilon) * weight


def local(
    seq_size,
    tokens,
    cotangent,
    norm_gain,
    in_weight,
    conv_weight,
    conv_bias,
    dt_bias,
    a_log,
    d_skip,
    gate_gain,
    out_weight,
):
    axes = ("dp", "seq")
    sizes = [norm_gain.shape[0], conv_weight.size, conv_bias.shape[0], gate_gain.shape[0]]
    packed = jnp.concatenate([norm_gain, conv_weight.reshape(-1), conv_bias, gate_gain])
    packed = lax.all_gather(packed[None].astype(f32), axes, axis=0, tiled=True)
    offsets = [0]
    for size in sizes:
        offsets.append(offsets[-1] + size)
    norm_full = packed[:, : offsets[1]].reshape(-1)
    taps_full = packed[:, offsets[1] : offsets[2]].reshape(-1, KCONV, conv_weight.shape[1])
    taps_full = jnp.swapaxes(taps_full, 0, 1).reshape(KCONV, DC)
    cbias_full = packed[:, offsets[2] : offsets[3]].reshape(1, DC)
    gain_full = packed[:, offsets[3] :].reshape(1, DI)
    in_full = lax.all_gather(in_weight, axes, axis=0, tiled=True)
    out_full = lax.all_gather(out_weight, axes, axis=0, tiled=True)
    heads = jnp.stack([dt_bias, a_log, d_skip])

    tokens = tokens[0]
    cotangent = cotangent[0]
    inputs = tokens.astype(f32)
    normed, norm_back = jax.vjp(rms_scale, inputs, norm_full)
    normed_low = normed.astype(bf16)
    proj = mm(normed_low, in_full).astype(bf16)
    grad_low = mm_nt(cotangent, out_full)
    gate_low, grad_proj, sum_conv, sum_gate, sum_head = ssd_call(
        seq_size, proj, grad_low, taps_full, cbias_full, heads, gain_full
    )
    block_out = (inputs + mm(gate_low, out_full)).astype(bf16)
    outward = lax.dot_general(
        gate_low, cotangent, (((0,), (0,)), ((), ())), preferred_element_type=f32
    )
    inward = lax.dot_general(
        normed_low, grad_proj, (((0,), (0,)), ((), ())), preferred_element_type=f32
    )
    grad_normed = mm_nt(grad_proj, in_full)
    grad_inputs, norm_local = norm_back(grad_normed)
    input_grad = (grad_inputs + cotangent.astype(f32)).astype(bf16)

    conv_local = jnp.sum(sum_conv.reshape(KCONV + 1, 8, DC), axis=1)
    gate_local = jnp.sum(sum_gate.reshape(2, 8, DI), axis=1)
    head_local = jnp.sum(sum_head.reshape(2, 8, LANES), axis=1)[:, :NHEADS]
    skip_local = jnp.sum(gate_local[1].reshape(NHEADS, HEADDIM), axis=1)
    inward = lax.psum_scatter(inward.astype(bf16), axes, scatter_dimension=0, tiled=True)
    outward = lax.psum_scatter(outward.astype(bf16), axes, scatter_dimension=0, tiled=True)
    small = lax.psum(
        jnp.concatenate(
            [norm_local, conv_local.reshape(-1), gate_local[0], head_local.reshape(-1), skip_local]
        ),
        axes,
    )
    rank = lax.axis_index("dp") * seq_size + lax.axis_index("seq")
    at = 0

    def take(count):
        nonlocal at
        at += count
        return small[at - count : at]

    def mine(values, like):
        return lax.dynamic_slice_in_dim(values, rank * like, like, values.ndim - 1)

    norm_grad = mine(take(norm_full.shape[0]), norm_gain.shape[0])
    kernel_grad = mine(take(KCONV * DC).reshape(KCONV, DC), conv_weight.shape[1])
    offset_grad = mine(take(DC), conv_bias.shape[0])
    gain_grad = mine(take(DI), gate_gain.shape[0])
    step_grad, decay_grad, skip_grad = take(NHEADS), take(NHEADS), take(NHEADS)
    return (
        block_out[None],
        input_grad[None],
        norm_grad,
        inward.astype(f32),
        kernel_grad,
        offset_grad,
        step_grad,
        decay_grad,
        skip_grad,
        gain_grad,
        outward.astype(f32),
    )


def solution(mesh):
    both = ("dp", "seq")
    return jax.shard_map(
        functools.partial(local, mesh.shape["seq"]),
        mesh=mesh,
        in_specs=(
            P("dp", "seq", None),
            P("dp", "seq", None),
            P(both),
            P(both, None),
            P(None, both),
            P(both),
            P(),
            P(),
            P(),
            P(both),
            P(both, None),
        ),
        out_specs=(
            P("dp", "seq", None),
            P("dp", "seq", None),
            P(both),
            P(both, None),
            P(None, both),
            P(both),
            P(),
            P(),
            P(),
            P(both),
            P(both, None),
        ),
        check_vma=False,
    )
```

profile of v0, /device:TPU:0, one launch (start us, length us, event | category | flops | bytes accessed | tf_op | source)
XLA Modules:
  0.0 440.6 jit_solution(4549557882022019264)
XLA Ops:
  7.2 0.7 all-gather.6.cloned.1.call-update
  7.9 0.0 all-gather.4.cloned.1.call-start
  8.0 0.7 all-gather.4.cloned.1.call-update
  8.7 0.0 reduce-scatter.5.cloned.1.call-start
  8.7 0.8 concatenate.22
  9.5 0.8 fusion.17
  10.2 43.4 %all-gather = f32[32,1,352]{2,1,0:T(1,128)S(1)} all-gather(f32[1,1,352]{2,1,0:T(1,128)S(1)} %fusion.17), channel_id=1, replica_groups=mesh['dp'=4,'seq'=8] {'dp','seq'}, dimensions={0}, use_global_device_ids=true | all-gather | bytes 46464 | tf_op jit(solution)/shard_map/all_gather | solution.py:665
  53.7 0.1 slice.57
  53.7 0.1 slice.58
  53.8 0.1 slice.59
  53.9 0.1 mul.74
  54.0 0.1 reshape.132
  54.1 0.7 reshape.133.taps
  54.8 0.7 reshape.134.cbias
  55.5 0.7 reshape.135.gain
  56.2 1.3 pad_maximum_fusion.heads
  57.4 1.4 fusion.6
  58.8 11.8 %all-gather.6.cloned.1.call-done = bf16[1536,768]{1,0:T(8,128)(2,1)} async-done(((bf16[48,768]{1,0:T(8,128)(2,1)}), bf16[1536,768]{1,0:T(8,128)(2,1)}) %all-gather.6.cloned.1.call-update) | async-done | bytes 2359312 | tf_op jit(solution)/shard_map/all_gather | solution.py:675
  70.6 4.7 %fusion.12.grad_low = f32[512,1536]{1,0:T(8,128)} fusion(bf16[1536,768]{1,0:T(8,128)(2,1)} %all-gather.6.cloned.1.call-done, bf16[1,512,768]{2,1,0:T(8,128)(2,1)S(1)} %copy-done.1), kind=kOutput, calls=%fused_computation.21 | convolution fusion | flops 1207959552 | bytes 6291456 | tf_op jit(solution)/shard_map/dot_general | solution.py:32
  75.3 62.6 %all-gather.4.cloned.1.call-done = bf16[768,3352]{1,0:T(8,128)(2,1)} async-done(((bf16[24,3352]{1,0:T(8,128)(2,1)}), bf16[768,3352]{1,0:T(8,128)(2,1)}) %all-gather.4.cloned.1.call-update) | async-done | bytes 5148688 | tf_op jit(solution)/shard_map/all_gather | solution.py:674
  137.9 5.7 %convolution_convert_fusion.1 = bf16[512,3352]{0,1:T(8,128)(2,1)S(1)} fusion(bf16[768,3352]{1,0:T(8,128)(2,1)} %all-gather.4.cloned.1.call-done, bf16[1,512,768]{2,1,0:T(8,128)(2,1)} %param.11, f32[768]{0:T(1024)S(1)} %mul.74, f32[512]{0:T(512)S(1)} %fusion.16), kind=kOutput, calls=%fused_computation.1 | convolution fusion | flops 2639409152 | bytes 9372672 | tf_op jit(solution)/shard_map/dot_general | solution.py:28
  143.7 3.7 copy.31.proj
  147.3 73.9 %ssd.1 = (bf16[512,1536]{1,0:T(8,128)(2,1)}, bf16[512,3352]{1,0:T(8,128)(2,1)}, f32[40,1792]{1,0:T(8,128)}, f32[16,1536]{1,0:T(8,128)}, f32[16,128]{1,0:T(8,128)}) custom-call(bf16[512,3352]{1,0:T(8,128)(2,1)} %copy.31.proj, f32[512,1536]{1,0:T(8,128)} %fusion.12.grad_low, f32[4,1792]{1,0:T(4,128)} %reshape.133.taps, f32[1,1792]{1,0:T(1,128)} %reshape.134.cbias, ...), custom_call_target="tpu_custom_call" | custom-call | tf_op jit(solution)/shard_map/ssd/pallas_call | solution.py:585
  221.3 4.2 convolution_convert_fusion.2
  225.5 0.3 reduce-scatter.7.cloned.1.call-start
  225.8 0.8 copy-done
  226.6 6.9 %convolution_convert_fusion = bf16[768,3352]{1,0:T(8,128)(2,1)} fusion(bf16[512,3352]{1,0:T(8,128)(2,1)} %get-tuple-element.17, bf16[1,512,768]{2,1,0:T(8,128)(2,1)S(1)} %copy-done, f32[768]{0:T(1024)S(1)} %mul.74, f32[512]{0:T(512)S(1)} %fusion.16), kind=kOutput, calls=%fused_computation | convolution fusion | flops 2640267264 | bytes 9372672 | tf_op jit(solution)/shard_map/dot_general | solution.py:692
  233.6 0.9 copy-done.4
  234.5 0.1 reshape_squeeze.3
  234.6 0.1 bitcast_reduce_fusion
  234.7 0.1 reshape.140
  234.8 0.1 reduce_sum.77
  234.9 7.0 %fusion.3 = (f32[768]{0:T(1024)S(1)}, f32[512]{0:T(512)S(1)}, f32[512,768]{1,0:T(8,128)S(1)}) fusion(bf16[1,512,768]{2,1,0:T(8,128)(2,1)S(1)} %copy-done, f32[512]{0:T(512)S(1)} %fusion.16, f32[768]{0:T(1024)S(1)} %mul.74, bf16[512,3352]{1,0:T(8,128)(2,1)} %get-tuple-element.17, bf16[768,3352]{1,0:T(8,128)(2,1)} %all-gather.4.cloned.1.call-done), kind=kOutput, calls=%fused_computation.12 | convolution fusion | flops 2638871296 | bytes 10950656 | tf_op jit(solution)/shard_map/dot_general | solution.py:32
  241.9 0.1 concatenate.26
  241.9 39.9 %psum.7 = f32[11336]{0:T(1024)S(1)} all-reduce(f32[11336]{0:T(1024)S(1)} %concatenate.26), channel_id=1, replica_groups=mesh['dp'=4,'seq'=8] {'dp','seq'}, use_global_device_ids=true, to_apply=%region_7.0 | all-reduce | flops 11336 | bytes 90688 | tf_op jit(solution)/shard_map/psum | solution.py:705
  281.9 0.6 dynamic_slice.14
  282.5 0.6 dynamic_slice.15
  283.1 0.6 dynamic_slice.12
  283.7 0.6 constant_dynamic-slice_fusion
  284.3 0.6 fusion.18
  284.9 1.4 fusion.10
  286.3 0.6 copy-done.6
  286.9 0.5 copy-done.7
  287.3 2.3 fusion.9
  289.6 34.5 %reduce-scatter.5.cloned.1.call-done = bf16[48,768]{1,0:T(8,128)(2,1)} async-done(((bf16[1536,768]{1,0:T(8,128)(2,1)}), bf16[48,768]{1,0:T(8,128)(2,1)}) %reduce-scatter.5.cloned.1.call-update) | async-done | bytes 73744 | tf_op jit(solution)/shard_map/reduce_scatter | solution.py:704
  324.1 1.6 convert_element_type.55
  325.7 106.7 %reduce-scatter.7.cloned.1.call-done = bf16[24,3352]{1,0:T(8,128)(2,1)} async-done(((bf16[768,3352]{1,0:T(8,128)(2,1)}), bf16[24,3352]{1,0:T(8,128)(2,1)}) %reduce-scatter.7.cloned.1.call-update) | async-done | bytes 160912
  432.4 1.7 convert_element_type.53
  (29 shorter events, 0.3 us)
Async XLA Ops:
  7.2 63.4 %copy-start.1 = (bf16[1,512,768]{2,1,0:T(8,128)(2,1)S(1)}, bf16[1,512,768]{2,1,0:T(8,128)(2,1)}, u32[]{:S(2)}) copy-start(bf16[1,512,768]{2,1,0:T(8,128)(2,1)} %param.12) | copy-start | bytes 2359300
  7.2 63.4 %all-gather.6.cloned.1.call-start = ((), (), s32[]{:S(2)}) async-start(), calls=%async_computation.3 | async-start | bytes 2433024 | tf_op jit(solution)/shard_map/all_gather | solution.py:675
  7.9 130.0 %all-gather.4.cloned.1.call-start = ((), (), s32[]{:S(2)}) async-start(), calls=%async_computation.2 | async-start | bytes 5474304 | tf_op jit(solution)/shard_map/all_gather | solution.py:674
  8.7 315.5 %reduce-scatter.5.cloned.1.call-start = ((), (), s32[]{:S(2)}) async-start(), calls=%async_computation.4 | async-start | bytes 2433024 | tf_op jit(solution)/shard_map/reduce_scatter | solution.py:704
  147.3 73.9 %copy-start.2 = (bf16[1,512,768]{2,1,0:T(8,128)(2,1)S(1)}, bf16[1,512,768]{2,1,0:T(8,128)(2,1)}, u32[]{:S(2)}) copy-start(bf16[1,512,768]{2,1,0:T(8,128)(2,1)} %param.12) | copy-start | bytes 2359300
  225.5 1.1 copy-start
  225.5 206.8 %reduce-scatter.7.cloned.1.call-start = ((), (), s32[]{:S(2)}) async-start(), calls=%async_computation.5 | async-start | bytes 5474304
  233.5 0.9 copy-start.4
  233.5 1.0 copy-start.3
  233.5 1.1 copy-start.5
  284.9 2.0 copy-start.6
  284.9 2.4 copy-start.7
Sparse Core Ops, SparseCore 0:
  10.9 59.6 all-gather.5
  73.5 64.3 all-gather.3
  225.6 98.4 reduce-scatter.4
  329.7 102.6 reduce-scatter.6
where the time goes:
time: 441 us
  waiting for transfers between devices  217 us (49%)
  blocking collectives  83.3 us (19%)
  Pallas kernels  73.9 us (17%)
  matrix products  30.8 us (7%)
  between operations  13.9 us (3%)
  local copies, waits for them, and re-layouts  13 us (3%)
  other arithmetic  8.26 us (2%)
    unnamed x5, waiting for transfers between devices  108 us
    pallas_call x1, Pallas kernels, ssd_call(): pl.pallas_call(functools.partial(ssd_kernel, seq_size), name='ssd', out_s...  73.9 us
    all_gather x1, waiting for transfers between devices, local(): in_full = lax.all_gather(in_weight, axes, axis=0, tiled=True)  62.6 us
    all_gather x1, blocking collectives, local(): packed = lax.all_gather(packed[None].astype(f32), axes, axis=0, tiled=True)  43.4 us
    psum x1, blocking collectives, local(): lax.psum(jnp.concatenate([norm_local, conv_local.reshape(-1), gate_local[...  39.9 us
    reduce_scatter x1, waiting for transfers between devices, local(): lax.psum_scatter(outward.astype(bf16), axes, scatter_dimension=0, tiled=T...  34.5 us
    all_gather x1, waiting for transfers between devices, local(): out_full = lax.all_gather(out_weight, axes, axis=0, tiled=True)  11.8 us
    dot_general x2, matrix products, mm_nt(): lax.dot_general(a, b, (((1,), (1,)), ((), ())), preferred_element_type=f32)  11.7 us
  transfers between devices with their start and end apart: 4, of which 4 were waited for; matrix products, arithmetic and copies ran while one was open for 8% of the time, Pallas kernels for 0%

commit v1 on v0

--- a/solution.py
+++ b/solution.py
@@ -641,11 +641,279 @@
     )(proj, grad_low, taps, cbias, heads, gain)
 
 
+def mesh_digits(sizes):
+    steps = [("seq", 1 << r, 2) for r in range(sizes["seq"].bit_length() - 1)]
+    first = [("dp", 1, sizes["dp"])]
+    return first + steps[1:] + steps[:1], first + steps[:0:-1] + steps[:1]
+
+
+def digit_of(digit):
+    axis, stride, size = digit
+    return (lax.axis_index(axis) // stride) % size
+
+
+def moved(digit, offset):
+    axis, stride, size = digit
+    now = digit_of(digit)
+    return lax.axis_index(axis) + ((now + offset) % size - now) * stride
+
+
+def rank_at(sizes, changes):
+    place = {axis: lax.axis_index(axis) for axis in sizes}
+    for digit, offset in changes:
+        axis, stride, size = digit
+        now = digit_of(digit)
+        place[axis] = place[axis] + ((now + offset) % size - now) * stride
+    return place["dp"] * sizes["seq"] + place["seq"]
+
+
+def greet(sizes):
+    barrier = pltpu.get_barrier_semaphore()
+    count = 0
+    for digit in mesh_digits(sizes)[0]:
+        for offset in range(1, digit[2]):
+            pl.semaphore_signal(
+                barrier, inc=1, device_id={digit[0]: moved(digit, offset)}, device_id_type=MESH
+            )
+            count += 1
+    pl.semaphore_wait(barrier, count)
+
+
+def spans(width, parts):
+    tiles = width // LANES
+    edges = [tiles * k // parts * LANES for k in range(parts)] + [width]
+    return [(edges[k], edges[k + 1] - edges[k]) for k in range(parts)]
+
+
+def gather_kernel(sizes, *refs):
+    items = 3
+    sources, targets = refs[:items], refs[items : 2 * items]
+    own_sems, sends, arrivals = refs[2 * items :]
+    greet(sizes)
+    orders = mesh_digits(sizes)
+    mine = rank_at(sizes, [])
+    for k in range(items):
+        pltpu.make_async_copy(sources[k], targets[k].at[mine], own_sems.at[k]).start()
+
+    streams = []
+    for k in range(items):
+        width = sources[k].shape[1]
+        for j, (at, size) in enumerate(spans(width, 2 if width > 512 else 1)):
+            streams.append((k, at, size, orders[j], len(streams)))
+    used = [0] * len(streams)
+    waits = []
+
+    def copy(stream, changes, digit, offset, first):
+        k, at, size, _, index = stream
+        slot = rank_at(sizes, changes)
+        lanes = pl.ds(at, size)
+        source = sources[k].at[:, lanes] if first else targets[k].at[slot, :, lanes]
+        return pltpu.make_async_remote_copy(
+            src_ref=source,
+            dst_ref=targets[k].at[slot, :, lanes],
+            send_sem=sends.at[index, used[index]],
+            recv_sem=arrivals.at[index, slot],
+            device_id={digit[0]: moved(digit, offset)},
+            device_id_type=MESH,
+        )
+
+    def pass_on(stream, changes, depth):
+        order = stream[3]
+        for position in range(depth, len(order)):
+            digit = order[position]
+            for offset in range(1, digit[2]):
+                started = copy(stream, changes, digit, offset, not changes)
+                used[stream[4]] += 1
+                started.start()
+                waits.append(started)
+
+    def arrived(stream, changes):
+        k, at, size, _, index = stream
+        slot = rank_at(sizes, changes)
+        lanes = pl.ds(at, size)
+        pltpu.make_async_remote_copy(
+            src_ref=targets[k].at[slot, :, lanes],
+            dst_ref=targets[k].at[slot, :, lanes],
+            send_sem=sends.at[index, 0],
+            recv_sem=arrivals.at[index, slot],
+            device_id={"dp": moved(orders[0][0], 1)},
+            device_id_type=MESH,
+        ).wait_recv()
+
+    def shards(order, depth):
+        found = [[]]
+        for position in range(depth):
+            found = [
+                held + ([(order[position], offset)] if offset else [])
+                for held in found
+                for offset in range(order[position][2])
+            ]
+        return [
+            held + [(order[depth], offset)] for held in found for offset in range(1, order[depth][2])
+        ]
+
+    for stream in streams:
+        pass_on(stream, [], 0)
+    for depth in range(len(orders[0])):
+        lists = [(stream, shards(stream[3], depth)) for stream in streams]
+        for turn in range(len(lists[0][1])):
+            for stream, held in lists:
+                arrived(stream, held[turn])
+                pass_on(stream, held[turn], depth + 1)
+    for started in waits:
+        started.wait_send()
+    for k in range(items):
+        pltpu.make_async_copy(sources[k], targets[k].at[mine], own_sems.at[k]).wait()
+
+
+def gather_call(sizes, *arrays):
+    count = sizes["dp"] * sizes["seq"]
+    streams = 5
+    return pl.pallas_call(
+        functools.partial(gather_kernel, sizes),
+        name="gather",
+        out_shape=tuple(jax.ShapeDtypeStruct((count,) + a.shape, a.dtype) for a in arrays),
+        in_specs=[pl.BlockSpec(memory_space=pltpu.VMEM)] * len(arrays),
+        out_specs=[pl.BlockSpec(memory_space=pl.ANY)] * len(arrays),
+        scratch_shapes=[
+            pltpu.SemaphoreType.DMA((len(arrays),)),
+            pltpu.SemaphoreType.DMA((streams, count)),
+            pltpu.SemaphoreType.DMA((streams, count)),
+        ],
+        compiler_params=pltpu.CompilerParams(collective_id=2, has_side_effects=True),
+    )(*arrays)
+
+
+def scatter_kernel(sizes, parts, items, *refs):
+    orders = mesh_digits(sizes)
+    depth = len(orders[0])
+    lengths = [digit[2] for digit in orders[0]]
+    counts = [1]
+    for size in lengths:
+        counts.append(counts[-1] * size)
+    sources, refs = refs[:items], refs[items:]
+    targets, refs = refs[:items], refs[items:]
+    sums, refs = refs[:items], refs[items:]
+    landed, refs = refs[: items * depth], refs[items * depth :]
+    sends, arrivals = refs
+    greet(sizes)
+
+    streams = []
+    for k in range(items):
+        for j, (at, size) in enumerate(spans(sources[k].shape[2], parts[k])):
+            streams.append((k, pl.ds(at, size), orders[j % 2], len(streams)))
+    base = [0]
+    for position in range(depth):
+        base.append(base[-1] + (lengths[position] - 1) * counts[position])
+    started, waiting = [], []
+
+    def offsets_of(relative):
+        found = []
+        for size in lengths:
+            found.append(relative % size)
+            relative //= size
+        return found
+
+    def copy(stream, position, offset, relative):
+        k, lanes, order, index = stream
+        digit = order[position]
+        if position == depth - 1:
+            changes = list(zip(order, offsets_of(relative) [:position] + [offset]))
+            source = sources[k].at[rank_at(sizes, changes), :, lanes]
+        else:
+            source = sums[k].at[offset * counts[position] + relative, :, lanes]
+        there = (digit[2] - offset - 1) * counts[position] + relative
+        return pltpu.make_async_remote_copy(
+            src_ref=source,
+            dst_ref=landed[k * depth + position].at[there, :, lanes],
+            send_sem=sends.at[index, base[position] + there],
+            recv_sem=arrivals.at[index, base[position] + there],
+            device_id={digit[0]: moved(digit, offset)},
+            device_id_type=MESH,
+        )
+
+    def flush(keep):
+        while len(waiting) > keep:
+            item = waiting.pop(0)
+            item.start()
+            started.append(item)
+
+    def receive(stream, position, relative):
+        k, lanes, order, index = stream
+        if position == depth - 1:
+            own = list(zip(order, offsets_of(relative)[:position]))
+            total = sources[k][rank_at(sizes, own), :, lanes].astype(f32)
+        else:
+            total = sums[k][relative, :, lanes].astype(f32)
+        buffer = landed[k * depth + position]
+        for offset in range(1, lengths[position]):
+            here = (offset - 1) * counts[position] + relative
+            pltpu.make_async_remote_copy(
+                src_ref=buffer.at[here, :, lanes],
+                dst_ref=buffer.at[here, :, lanes],
+                send_sem=sends.at[index, base[position] + here],
+                recv_sem=arrivals.at[index, base[position] + here],
+                device_id={order[position][0]: moved(order[position], offset)},
+                device_id_type=MESH,
+            ).wait_recv()
+            total += buffer[here, :, lanes].astype(f32)
+        if position == 0:
+            targets[k][:, lanes] = total
+            return
+        sums[k][relative, :, lanes] = total.astype(sums[k].dtype)
+        offset, below = divmod(relative, counts[position - 1])
+        if offset:
+            waiting.append(copy(stream, position - 1, offset, below))
+
+    for relative in reversed(range(counts[depth - 1])):
+        for stream in streams:
+            for offset in range(1, lengths[depth - 1]):
+                waiting.append(copy(stream, depth - 1, offset, relative))
+                flush(0)
+    for position in reversed(range(depth)):
+        for relative in reversed(range(counts[position])):
+            for stream in streams:
+                receive(stream, position, relative)
+                flush(1)
+        flush(0)
+    for item in started:
+        item.wait_send()
+
+
+def scatter_call(sizes, parts, *arrays):
+    depth = sizes["seq"].bit_length()
+    lengths = [sizes["dp"]] + [2] * (depth - 1)
+    counts = [1]
+    for size in lengths:
+        counts.append(counts[-1] * size)
+    most = sum((lengths[j] - 1) * counts[j] for j in range(depth))
+    scratch = [pltpu.VMEM((counts[depth - 1],) + a.shape[1:], a.dtype) for a in arrays]
+    for a in arrays:
+        for j in range(depth):
+            scratch.append(pltpu.VMEM(((lengths[j] - 1) * counts[j],) + a.shape[1:], a.dtype))
+    return pl.pallas_call(
+        functools.partial(scatter_kernel, sizes, parts, len(arrays)),
+        name="scatter",
+        out_shape=tuple(jax.ShapeDtypeStruct(a.shape[1:], f32) for a in arrays),
+        in_specs=[pl.BlockSpec(memory_space=pltpu.VMEM)] * len(arrays),
+        out_specs=[pl.BlockSpec(memory_space=pltpu.VMEM)] * len(arrays),
+        scratch_shapes=scratch
+        + [
+            pltpu.SemaphoreType.DMA((sum(parts), most)),
+            pltpu.SemaphoreType.DMA((sum(parts), most)),
+        ],
+        compiler_params=pltpu.CompilerParams(
+            collective_id=3, has_side_effects=True, vmem_limit_bytes=62 * 1024 * 1024
+        ),
+    )(*arrays)
+
+
 def rms_scale(values, weight):
     return values * lax.rsqrt(jnp.mean(values * values, axis=-1, keepdims=True) + epsilon) * weight
 
 
 def local(
+    dp_size,
     seq_size,
     tokens,
     cotangent,
@@ -662,7 +930,12 @@
     axes = ("dp", "seq")
     sizes = [norm_gain.shape[0], conv_weight.size, conv_bias.shape[0], gate_gain.shape[0]]
     packed = jnp.concatenate([norm_gain, conv_weight.reshape(-1), conv_bias, gate_gain])
-    packed = lax.all_gather(packed[None].astype(f32), axes, axis=0, tiled=True)
+    in_full, out_full, packed = gather_call(
+        {"dp": dp_size, "seq": seq_size}, in_weight, out_weight, packed[None].astype(f32)
+    )
+    in_full = in_full.reshape(-1, in_weight.shape[1])
+    out_full = out_full.reshape(-1, out_weight.shape[1])
+    packed = packed[:, 0]
     offsets = [0]
     for size in sizes:
         offsets.append(offsets[-1] + size)
@@ -671,8 +944,6 @@
     taps_full = jnp.swapaxes(taps_full, 0, 1).reshape(KCONV, DC)
     cbias_full = packed[:, offsets[2] : offsets[3]].reshape(1, DC)
     gain_full = packed[:, offsets[3] :].reshape(1, DI)
-    in_full = lax.all_gather(in_weight, axes, axis=0, tiled=True)
-    out_full = lax.all_gather(out_weight, axes, axis=0, tiled=True)
     heads = jnp.stack([dt_bias, a_log, d_skip])
 
     tokens = tokens[0]
@@ -700,49 +971,49 @@
     gate_local = jnp.sum(sum_gate.reshape(2, 8, DI), axis=1)
     head_local = jnp.sum(sum_head.reshape(2, 8, LANES), axis=1)[:, :NHEADS]
     skip_local = jnp.sum(gate_local[1].reshape(NHEADS, HEADDIM), axis=1)
-    inward = lax.psum_scatter(inward.astype(bf16), axes, scatter_dimension=0, tiled=True)
-    outward = lax.psum_scatter(outward.astype(bf16), axes, scatter_dimension=0, tiled=True)
-    small = lax.psum(
-        jnp.concatenate(
-            [norm_local, conv_local.reshape(-1), gate_local[0], head_local.reshape(-1), skip_local]
-        ),
-        axes,
+    count = dp_size * seq_size
+    shared = jnp.concatenate([head_local.reshape(-1), skip_local])
+    pieces = [
+        norm_local.reshape(count, -1),
+        jnp.swapaxes(conv_local[:KCONV].reshape(KCONV, count, -1), 0, 1).reshape(count, -1),
+        conv_local[KCONV].reshape(count, -1),
+        gate_local[0].reshape(count, -1),
+        jnp.broadcast_to(shared[None], (count, shared.shape[0])),
+    ]
+    widths = [piece.shape[1] for piece in pieces]
+    width = -(-sum(widths) // LANES) * LANES
+    pieces.append(jnp.zeros((count, width - sum(widths)), f32))
+    inward, outward, small = scatter_call(
+        {"dp": dp_size, "seq": seq_size},
+        (4, 2, 1),
+        inward.astype(bf16).reshape(count, -1, inward.shape[1]),
+        outward.astype(bf16).reshape(count, -1, outward.shape[1]),
+        jnp.concatenate(pieces, axis=1)[:, None],
     )
-    rank = lax.axis_index("dp") * seq_size + lax.axis_index("seq")
-    at = 0
-
-    def take(count):
-        nonlocal at
-        at += count
-        return small[at - count : at]
-
-    def mine(values, like):
-        return lax.dynamic_slice_in_dim(values, rank * like, like, values.ndim - 1)
-
-    norm_grad = mine(take(norm_full.shape[0]), norm_gain.shape[0])
-    kernel_grad = mine(take(KCONV * DC).reshape(KCONV, DC), conv_weight.shape[1])
-    offset_grad = mine(take(DC), conv_bias.shape[0])
-    gain_grad = mine(take(DI), gate_gain.shape[0])
-    step_grad, decay_grad, skip_grad = take(NHEADS), take(NHEADS), take(NHEADS)
+    at = [sum(widths[:k]) for k in range(6)]
+    parts = [small[0, at[k] : at[k + 1]] for k in range(5)]
+    norm_grad, kernel_grad, offset_grad, gain_grad, shared = parts
+    kernel_grad = kernel_grad.reshape(KCONV, -1)
+    step_grad, decay_grad, skip_grad = shared.reshape(3, NHEADS)
     return (
         block_out[None],
         input_grad[None],
         norm_grad,
-        inward.astype(f32),
+        inward,
         kernel_grad,
         offset_grad,
         step_grad,
         decay_grad,
         skip_grad,
         gain_grad,
-        outward.astype(f32),
+        outward,
     )
 
 
 def solution(mesh):
     both = ("dp", "seq")
     return jax.shard_map(
-        functools.partial(local, mesh.shape["seq"]),
+        functools.partial(local, mesh.shape["dp"], mesh.shape["seq"]),
         mesh=mesh,
         in_specs=(
             P("dp", "seq", None),

time: 441 us -> 254 us (0.58)
  waiting for transfers between devices: 217 us -> 0 us
  Pallas kernels: 73.9 us -> 188 us
  blocking collectives: 83.3 us -> 0 us
  between operations: 13.9 us -> 0.82 us
  local copies, waits for them, and re-layouts: 13 us -> 23.7 us
    pallas_call x0 -> x2, Pallas kernels: none -> 114 us  [the longest x1 63.9 us: scatter_call(): pl.pallas_call(functools.partial(scatter_kernel, sizes, parts, len(arrays...]
    unnamed x5 -> x0, waiting for transfers between devices: 108 us -> none
    all_gather x2 -> x0, waiting for transfers between devices: 74.4 us -> none  [the longest x1 62.6 us: local(): in_full = lax.all_gather(in_weight, axes, axis=0, tiled=True)]
    all_gather x1 -> x0, blocking collectives: 43.4 us -> none  [local(): packed = lax.all_gather(packed[None].astype(f32), axes, axis=0, tiled=True)]
    psum x1 -> x0, blocking collectives: 39.9 us -> none  [local(): lax.psum(jnp.concatenate([norm_local, conv_local.reshape(-1), gate_local[...]
    reduce_scatter x1 -> x0, waiting for transfers between devices: 34.5 us -> none  [local(): lax.psum_scatter(outward.astype(bf16), axes, scatter_dimension=0, tiled=T...]
    convert_element_type x0 -> x1, local copies, waits for them, and re-layouts: none -> 7.96 us  [local(): inward.astype(bf16).reshape(count, -1, inward.shape[1])]
  transfers between devices with their start and end apart: 4 -> 0, of which waited for: 4 -> 0; matrix products, arithmetic and copies ran while one was open for 8% -> 0% of each run, Pallas kernels for 0% -> 0%
where the time goes in v1:
time: 254 us; the launch traced here: 253 us
  Pallas kernels  188 us (74%)
  matrix products  32.4 us (13%)
  local copies, waits for them, and re-layouts  23.7 us (9%)
  other arithmetic  8.14 us (3%)
    pallas_call x1, Pallas kernels, ssd_call(): pl.pallas_call(functools.partial(ssd_kernel, seq_size), name='ssd', out_s...  74.4 us
    pallas_call x1, Pallas kernels, scatter_call(): pl.pallas_call(functools.partial(scatter_kernel, sizes, parts, len(arrays...  63.9 us
    pallas_call x1, Pallas kernels, gather_call(): pl.pallas_call(functools.partial(gather_kernel, sizes), name='gather', ou...  49.8 us
    dot_general x2, matrix products, mm_nt(): lax.dot_general(a, b, (((1,), (1,)), ((), ())), preferred_element_type=f32)  12.9 us
    dot_general x2, matrix products, mm(): lax.dot_general(a, b, (((1,), (0,)), ((), ())), preferred_element_type=f32)  7.99 us
    convert_element_type x1, local copies, waits for them, and re-layouts, local(): inward.astype(bf16).reshape(count, -1, inward.shape[1])  7.96 us
    dot_general x1, matrix products, local(): lax.dot_general(normed_low, grad_proj, (((0,), (0,)), ((), ())), preferre...  7.26 us

profile of v1, /device:TPU:0, one launch (start us, length us, event | category | flops | bytes accessed | tf_op | source)
XLA Modules:
  0.0 253.2 jit_solution(16213858275461113845)
XLA Ops:
  0.6 0.8 concatenate.25
  1.4 1.3 maximum_convert_fusion.refs_2_
  2.7 49.8 %gather.1 = (bf16[32,24,3352]{2,1,0:T(8,128)(2,1)}, bf16[32,48,768]{2,1,0:T(8,128)(2,1)}, f32[32,1,352]{2,1,0:T(1,128)}) custom-call(bf16[24,3352]{1,0:T(8,128)(2,1)} %refs_0_.1, bf16[48,768]{1,0:T(8,128)(2,1)} %refs_1_.1, f32[1,352]{1,0:T(1,128)} %maximum_convert_fusion.refs_2_), custom_call_target="tpu_custom_call" | custom-call | tf_op jit(solution)/shard_map/gather/pallas_call | solution.py:772
  52.5 0.8 copy.44
  53.3 0.1 mul.71
  53.4 1.4 fusion.9
  54.8 5.7 %convolution_convert_fusion.1 = bf16[512,3352]{0,1:T(8,128)(2,1)S(1)} fusion(bf16[768,3352]{1,0:T(8,128)(2,1)} %bitcast.113, bf16[1,512,768]{2,1,0:T(8,128)(2,1)} %param.11, f32[768]{0:T(1024)S(1)} %mul.71, f32[512]{0:T(512)S(1)} %fusion.27), kind=kOutput, calls=%fused_computation.1 | convolution fusion | flops 2639409152 | bytes 9372672 | tf_op jit(solution)/shard_map/dot_general | solution.py:28
  60.5 3.6 %copy.34.proj = bf16[512,3352]{1,0:T(8,128)(2,1)} copy(bf16[512,3352]{0,1:T(8,128)(2,1)S(1)} %convolution_convert_fusion.1) | data formatting | bytes 6864896 | tf_op jit(solution)/shard_map/convert_element_type | solution.py:954
  64.2 0.1 slice.60
  64.2 0.1 reshape.171
  64.3 0.7 reshape.172.taps
  65.1 0.1 slice.61
  65.1 0.7 reshape.173.cbias
  65.8 0.1 slice.62
  65.9 0.7 reshape.174.gain
  66.6 4.9 %convolution_bitcast_fusion.grad_low = f32[512,1536]{1,0:T(8,128)} fusion(bf16[1536,768]{1,0:T(8,128)(2,1)} %bitcast.115, bf16[1,512,768]{2,1,0:T(8,128)(2,1)} %param.12), kind=kOutput, calls=%fused_computation.3 | convolution fusion | flops 1207959552 | bytes 6291456 | tf_op jit(solution)/shard_map/dot_general | solution.py:32
  71.5 0.0 copy-done.6
  71.5 0.6 pad_maximum_fusion.heads
  72.1 74.4 %ssd.1 = (bf16[512,1536]{1,0:T(8,128)(2,1)}, bf16[512,3352]{1,0:T(8,128)(2,1)}, f32[40,1792]{1,0:T(8,128)}, f32[16,1536]{1,0:T(8,128)}, f32[16,128]{1,0:T(8,128)}) custom-call(bf16[512,3352]{1,0:T(8,128)(2,1)} %copy.34.proj, f32[512,1536]{1,0:T(8,128)} %convolution_bitcast_fusion.grad_low, f32[4,1792]{1,0:T(4,128)} %reshape.172.taps, ...), custom_call_target="tpu_custom_call" | custom-call | tf_op jit(solution)/shard_map/ssd/pallas_call | solution.py:585
  146.5 0.9 bitcast_reduce_fusion.1
  147.5 0.1 reshape_squeeze.15
  147.6 0.1 reduce_sum.77
  147.7 0.7 bitcast_reduce_fusion.2
  148.4 0.1 reshape.183
  148.5 0.1 pad_maximum_fusion.1
  148.6 8.0 %fusion.8 = (f32[768]{0:T(1024)S(1)}, f32[512]{0:T(512)S(1)}, f32[512,768]{1,0:T(8,128)}) fusion(bf16[1,512,768]{2,1,0:T(8,128)(2,1)S(1)} %copy-done, f32[512]{0:T(512)S(1)} %fusion.27, f32[768]{0:T(1024)S(1)} %mul.71, bf16[512,3352]{1,0:T(8,128)(2,1)} %get-tuple-element.26, bf16[768,3352]{1,0:T(8,128)(2,1)} %bitcast.114), kind=kOutput, calls=%fused_computation.15 | convolution fusion | flops 2638871296 | bytes 10950656 | tf_op jit(solution)/shard_map/dot_general | solution.py:32
  156.5 0.1 reshape.177
  156.6 0.1 bitcast_reduce_fusion
  156.7 0.1 reshape.179
  156.9 0.1 reshape.180
  157.0 0.1 reshape_squeeze.13
  157.1 0.1 reshape_squeeze.14
  157.2 0.1 concatenate.30
  157.3 0.7 broadcast_in_dim.28.refs_2_
  158.0 7.3 %convolution_convert_fusion = bf16[768,3352]{0,1:T(8,128)(2,1)} fusion(bf16[512,3352]{1,0:T(8,128)(2,1)} %get-tuple-element.26, bf16[1,512,768]{2,1,0:T(8,128)(2,1)S(1)} %copy-done, f32[512]{0:T(512)S(1)} %fusion.27, f32[768]{0:T(1024)S(1)} %mul.71), kind=kOutput, calls=%fused_computation | convolution fusion | flops 2640267264 | bytes 9372672 | tf_op jit(solution)/shard_map/dot_general | solution.py:963
  165.2 8.0 %copy.35 = bf16[768,3352]{1,0:T(8,128)(2,1)} copy(bf16[768,3352]{0,1:T(8,128)(2,1)} %convolution_convert_fusion) | data formatting | bytes 10297344 | tf_op jit(solution)/shard_map/convert_element_type | solution.py:989
  173.2 4.3 %convolution_convert_fusion.2 = bf16[1536,768]{1,0:T(8,128)(2,1)} fusion(bf16[512,1536]{1,0:T(8,128)(2,1)} %get-tuple-element.25, bf16[1,512,768]{2,1,0:T(8,128)(2,1)S(1)} %copy-done.1), kind=kOutput, calls=%fused_computation.2 | convolution fusion | flops 1209139200 | bytes 4718592 | tf_op jit(solution)/shard_map/dot_general | solution.py:960
  177.5 63.9 %scatter.1 = (f32[24,3352]{1,0:T(8,128)}, f32[48,768]{1,0:T(8,128)}, f32[1,512]{1,0:T(1,128)}) custom-call(bf16[32,24,3352]{2,1,0:T(8,128)(2,1)} %bitcast.98, bf16[32,48,768]{2,1,0:T(8,128)(2,1)} %bitcast.99, f32[32,1,512]{2,1,0:T(1,128)} %broadcast_in_dim.28.refs_2_), custom_call_target="tpu_custom_call" | custom-call | tf_op jit(solution)/shard_map/scatter/pallas_call | solution.py:894
  241.4 0.8 slice_reduce_fusion.3
  242.2 0.7 reshape_squeeze.16
  242.8 1.3 slice_bitcast_fusion.1
  244.2 1.2 slice_bitcast_fusion
  245.3 1.3 slice_bitcast_fusion.4
  246.6 0.0 copy-start.9
  246.6 2.9 %fusion.17 = bf16[1,512,768]{2,1,0:T(8,128)(2,1)} fusion(bf16[1,512,768]{2,1,0:T(8,128)(2,1)S(1)} %copy-done, f32[512,768]{1,0:T(8,128)} %get-tuple-element.41, bf16[1,512,768]{2,1,0:T(8,128)(2,1)S(1)} %copy-done.1, f32[512]{0:T(512)S(1)} %multiply_multiply_fusion, f32[512]{0:T(512)S(1)} %fusion.27, f32[768]{0:T(1024)S(1)} %mul.71), kind=kLoop, calls=%fused_computation.24 | loop fusion | flops 3538944 | bytes 3939328 | tf_op jit(solution)/shard_map/broadcast_in_dim | solution.py:1000
  249.5 2.3 fusion.16
  251.8 0.7 copy.47
  252.5 0.7 copy.48
  (28 shorter events, 0.2 us)
Async XLA Ops:
  66.6 4.9 %copy-start.5 = (f32[24]{0:T(128)S(1)}, f32[24]{0:T(128)}, u32[]{:S(2)}) copy-start(f32[24]{0:T(128)} %param.19) | copy-start | bytes 292
  66.6 4.9 %copy-start.6 = (f32[24]{0:T(128)S(1)}, f32[24]{0:T(128)}, u32[]{:S(2)}) copy-start(f32[24]{0:T(128)} %param.18) | copy-start | bytes 292
  66.6 4.9 %copy-start.7 = (f32[24]{0:T(128)S(1)}, f32[24]{0:T(128)}, u32[]{:S(2)}) copy-start(f32[24]{0:T(128)} %param.17) | copy-start | bytes 292
  72.1 76.5 %copy-start = (bf16[1,512,768]{2,1,0:T(8,128)(2,1)S(1)}, bf16[1,512,768]{2,1,0:T(8,128)(2,1)}, u32[]{:S(2)}) copy-start(bf16[1,512,768]{2,1,0:T(8,128)(2,1)} %param.11) | copy-start | bytes 2359300
  148.6 8.0 %copy-start.3 = (f32[40,1792]{1,0:T(8,128)S(1)}, f32[40,1792]{1,0:T(8,128)}, u32[]{:S(2)}) copy-start(f32[40,1792]{1,0:T(8,128)} %get-tuple-element.27) | copy-start | bytes 860164
  165.2 8.0 %copy-start.1 = (bf16[1,512,768]{2,1,0:T(8,128)(2,1)S(1)}, bf16[1,512,768]{2,1,0:T(8,128)(2,1)}, u32[]{:S(2)}) copy-start(bf16[1,512,768]{2,1,0:T(8,128)(2,1)} %param.12) | copy-start | bytes 2359300
  246.6 2.9 %copy-start.8 = (bf16[32,48,768]{2,1,0:T(8,128)(2,1)S(1)}, bf16[32,48,768]{2,1,0:T(8,128)(2,1)}, u32[]{:S(2)}) copy-start(bf16[32,48,768]{2,1,0:T(8,128)(2,1)} %get-tuple-element.24) | copy-start | bytes 7077892
  246.6 2.9 %copy-start.9 = (bf16[512,1536]{1,0:T(8,128)(2,1)S(1)}, bf16[512,1536]{1,0:T(8,128)(2,1)}, u32[]{:S(2)}) copy-start(bf16[512,1536]{1,0:T(8,128)(2,1)} %get-tuple-element.25) | copy-start | bytes 4718596
  249.5 2.3 copy-start.2
  249.5 3.0 %copy-start.4 = (f32[48,768]{1,0:T(8,128)S(1)}, f32[48,768]{1,0:T(8,128)}, u32[]{:S(2)}) copy-start(f32[48,768]{1,0:T(8,128)} %get-tuple-element.63) | copy-start | bytes 442372

commit v2 on v1

--- a/solution.py
+++ b/solution.py
@@ -908,6 +908,517 @@
     )(*arrays)
 
 
+class Place:
+    def __init__(self):
+        self.z = lax.axis_index("dp")
+        seq = lax.axis_index("seq")
+        self.seq = seq
+        self.y = seq // 4
+        self.x = (seq // 2) % 2
+        self.c = seq % 2
+        self.over_x = {"seq": seq + 2 - 4 * self.x}
+        self.over_y = {"seq": seq + 4 - 8 * self.y}
+        self.sibling = {"seq": seq + 1 - 2 * self.c}
+        near = self.z < 2
+        self.mate = self.z + 1 - 2 * (self.z % 2)
+        self.planes = [self.z, self.mate, jnp.where(near, 2, 1), jnp.where(near, 3, 0)]
+        self.inner = jnp.logical_or(self.z == 1, self.z == 2)
+        self.across = 3 - self.z
+
+    def slot(self, o=0, y=0, x=0, c=0):
+        across = self.seq
+        across = across + (4 - 8 * self.y if y else 0)
+        across = across + (2 - 4 * self.x if x else 0)
+        across = across + (1 - 2 * self.c if c else 0)
+        return self.planes[o] * 8 + across
+
+    def greet(self):
+        barrier = pltpu.get_barrier_semaphore()
+        for other in (self.over_x, self.over_y, self.sibling):
+            pl.semaphore_signal(barrier, inc=1, device_id=other, device_id_type=MESH)
+        for o in range(1, 4):
+            pl.semaphore_signal(
+                barrier, inc=1, device_id={"dp": self.planes[o]}, device_id_type=MESH
+            )
+        pl.semaphore_wait(barrier, 6)
+
+
+def remote(source, target, send, arrival, device):
+    return pltpu.make_async_remote_copy(
+        src_ref=source,
+        dst_ref=target,
+        send_sem=send,
+        recv_sem=arrival,
+        device_id=device,
+        device_id_type=MESH,
+    )
+
+
+class Gather:
+    SENDS = 37
+
+    def __init__(self, place, source, target, sends, arrivals, cut):
+        self.place = place
+        self.source = source
+        self.target = target
+        self.sends = sends
+        self.arrivals = arrivals
+        width = source.shape[-1]
+        self.halves = (pl.ds(0, cut), pl.ds(cut, width - cut)) if cut else (pl.ds(0, width),) * 2
+        self.split = cut > 0
+        self.started = []
+
+    def send(self, slot, device, half=None, own=False, when=None):
+        at = self.target(slot)
+        start = self.source if own else at
+        part = 0
+        if half is not None:
+            if not self.split and half == 1:
+                return
+            part = half
+            start, at = start.at[:, self.halves[half]], at.at[:, self.halves[half]]
+        k = len(self.started)
+        copy = remote(start, at, self.sends.at[k], self.arrivals.at[slot, part], device)
+        if when is None:
+            copy.start()
+        else:
+            pl.when(when)(copy.start)
+        self.started.append((copy, when))
+
+    def wait(self, slot, half=None):
+        at = self.target(slot)
+        part = 0
+        if half is not None:
+            if not self.split and half == 1:
+                return
+            part = half
+            at = at.at[:, self.halves[half]]
+        remote(at, at, self.sends.at[0], self.arrivals.at[slot, part], self.place.sibling).wait_recv()
+
+    def spread(self, o, own=False):
+        place = self.place
+        slot = place.slot(o)
+        self.send(slot, place.over_x, own=own)
+        self.send(slot, place.over_y, own=own)
+        self.send(slot, place.sibling, own=own)
+
+    def start(self):
+        self.send(self.place.slot(), {"dp": self.place.mate}, own=True)
+        self.inward(0, self.place.across, own=True)
+        self.spread(0, own=True)
+
+    def inward(self, o, plane, own=False):
+        place = self.place
+        self.send(place.slot(o), {"dp": plane}, own=own, when=place.inner)
+
+    def steps(self):
+        place = self.place
+
+        def plane(o):
+            self.wait(place.slot(o))
+            self.inward(o, place.across if o == 1 else place.mate)
+            self.spread(o)
+
+        def side(o):
+            slot = place.slot(o, x=1)
+            self.wait(slot)
+            self.send(slot, place.over_y, half=0)
+            self.send(slot, place.sibling)
+            slot = place.slot(o, y=1)
+            self.wait(slot)
+            self.send(slot, place.over_x, half=1)
+            self.send(slot, place.sibling)
+
+        def corner(o):
+            slot = place.slot(o, x=1, y=1)
+            self.wait(slot, half=0)
+            self.wait(slot, half=1)
+            self.send(slot, place.sibling)
+
+        order = [(plane, 1), (side, 0), (plane, 2), (corner, 0), (side, 1), (plane, 3), (corner, 1)]
+        order += [(side, 2), (corner, 2), (side, 3), (corner, 3)]
+        return [functools.partial(step, o) for step, o in order] + [self.core]
+
+    def core(self):
+        for o in range(4):
+            for y in range(2):
+                for x in range(2):
+                    self.wait(self.place.slot(o, y, x, 1))
+
+    def drain(self):
+        for copy, when in self.started:
+            if when is None:
+                copy.wait_send()
+            else:
+                pl.when(when)(copy.wait_send)
+
+
+def quick_gather_kernel(*refs):
+    items = 3
+    sources, targets = refs[:items], refs[items : 2 * items]
+    own_sems = refs[2 * items]
+    sems = refs[2 * items + 1 :]
+    place = Place()
+    place.greet()
+    gathers = []
+    for k in range(items):
+        width = sources[k].shape[1]
+        cut = width // (2 * LANES) * LANES if width > 512 else 0
+        gathers.append(
+            Gather(place, sources[k], targets[k].at.__getitem__, sems[2 * k], sems[2 * k + 1], cut)
+        )
+    mine = place.slot()
+    for k in range(items):
+        pltpu.make_async_copy(sources[k], targets[k].at[mine], own_sems.at[k]).start()
+        gathers[k].start()
+    for steps in zip(*(gather.steps() for gather in gathers)):
+        for step in steps:
+            step()
+    for k in range(items):
+        gathers[k].drain()
+        pltpu.make_async_copy(sources[k], targets[k].at[mine], own_sems.at[k]).wait()
+
+
+def quick_gather_call(*arrays):
+    count = 32
+    sems = []
+    for _ in arrays:
+        sems += [pltpu.SemaphoreType.DMA((Gather.SENDS,)), pltpu.SemaphoreType.DMA((count, 2))]
+    return pl.pallas_call(
+        quick_gather_kernel,
+        name="gather",
+        out_shape=tuple(jax.ShapeDtypeStruct((count,) + a.shape, a.dtype) for a in arrays),
+        in_specs=[pl.BlockSpec(memory_space=pltpu.VMEM)] * len(arrays),
+        out_specs=[pl.BlockSpec(memory_space=pl.ANY)] * len(arrays),
+        scratch_shapes=[pltpu.SemaphoreType.DMA((len(arrays),))] + sems,
+        compiler_params=pltpu.CompilerParams(collective_id=5, has_side_effects=True),
+    )(*arrays)
+
+
+class Reduce:
+    def __init__(self, place, refs, cut):
+        self.place = place
+        (self.part, self.sums, self.land_c, self.land_x, self.land_y, self.land_xy, self.land_z) = refs[:7]
+        (self.sems_c, self.sems_a, self.sems_b, self.sems_z) = refs[7:]
+        width = self.part.shape[-1]
+        self.halves = (pl.ds(0, cut), pl.ds(cut, width - cut))
+
+    @staticmethod
+    def scratch(rows, width, cut, kind):
+        vmem = lambda *shape: pltpu.VMEM(shape + (rows, width), kind)
+        half = lambda size: pltpu.VMEM((4, 2, rows, size), kind)
+        dma = pltpu.SemaphoreType.DMA
+        return [
+            vmem(4, 2, 2, 2),
+            vmem(4, 2, 2),
+            vmem(4, 2, 2),
+            half(cut),
+            half(width - cut),
+            vmem(4),
+            vmem(4),
+            dma((4, 2)),
+            dma((4, 2, 2)),
+            dma((4, 2, 2)),
+            dma((4, 2)),
+        ]
+
+    def copy_c(self, o):
+        z, place = self.place.planes[o], self.place
+        return remote(
+            self.part.at[z, :, :, 1 - place.c],
+            self.land_c.at[z],
+            self.sems_c.at[z, 0],
+            self.sems_c.at[z, 1],
+            place.sibling,
+        )
+
+    def copy_first(self, o, half):
+        z, place = self.place.planes[o], self.place
+        lanes = self.halves[half]
+        if half == 0:
+            source, target = self.sums.at[z, :, 1 - place.x, :, lanes], self.land_x.at[z]
+        else:
+            source, target = self.sums.at[z, 1 - place.y, :, :, lanes], self.land_y.at[z]
+        device = place.over_y if half else place.over_x
+        return remote(source, target, self.sems_a.at[z, half, 0], self.sems_a.at[z, half, 1], device)
+
+    def copy_second(self, o, half):
+        z, place = self.place.planes[o], self.place
+        lanes = self.halves[half]
+        y, x = (place.y, 1 - place.x) if half else (1 - place.y, place.x)
+        device = place.over_x if half else place.over_y
+        return remote(
+            self.sums.at[z, y, x, :, lanes],
+            self.land_xy.at[z, :, lanes],
+            self.sems_b.at[z, half, 0],
+            self.sems_b.at[z, half, 1],
+            device,
+        )
+
+    def copy_plane(self, o):
+        place = self.place
+        z = place.planes[o]
+        return remote(
+            self.sums.at[z, place.y, place.x],
+            self.land_z.at[place.z],
+            self.sems_z.at[z, 0],
+            self.sems_z.at[place.z, 1],
+            {"dp": z},
+        )
+
+    def give(self, o):
+        self.copy_c(o).start()
+
+    def cores(self, o):
+        place, z = self.place, self.place.planes[o]
+        self.copy_c(o).wait_recv()
+        for y in range(2):
+            for x in range(2):
+                own = self.part[z, y, x, place.c].astype(f32)
+                self.sums[z, y, x] = (own + self.land_c[z, y, x].astype(f32)).astype(self.sums.dtype)
+        self.copy_first(o, 0).start()
+        self.copy_first(o, 1).start()
+
+    def firsts(self, o):
+        place, z = self.place, self.place.planes[o]
+        for half in range(2):
+            lanes = self.halves[half]
+            self.copy_first(o, half).wait_recv()
+            landed = self.land_y if half else self.land_x
+            for k in range(2):
+                y, x = (place.y, k) if half else (k, place.x)
+                own = self.sums[z, y, x, :, lanes].astype(f32)
+                self.sums[z, y, x, :, lanes] = (own + landed[z, k].astype(f32)).astype(
+                    self.sums.dtype
+                )
+            self.copy_second(o, half).start()
+
+    def seconds(self, o):
+        place, z = self.place, self.place.planes[o]
+        self.copy_second(o, 0).wait_recv()
+        self.copy_second(o, 1).wait_recv()
+        own = self.sums[z, place.y, place.x].astype(f32)
+        total = own + self.land_xy[z].astype(f32)
+        if o == 0:
+            return total
+        self.sums[z, place.y, place.x] = total.astype(self.sums.dtype)
+        self.copy_plane(o).start()
+
+    def last(self, total, target):
+        for o in range(1, 4):
+            z = self.place.planes[o]
+            remote(
+                self.land_z.at[z],
+                self.land_z.at[z],
+                self.sems_z.at[z, 0],
+                self.sems_z.at[z, 1],
+                {"dp": z},
+            ).wait_recv()
+            total += self.land_z[z].astype(f32)
+        target[...] = total
+
+    def drain(self):
+        for o in range(4):
+            self.copy_c(o).wait_send()
+            for half in range(2):
+                self.copy_first(o, half).wait_send()
+                self.copy_second(o, half).wait_send()
+            if o:
+                self.copy_plane(o).wait_send()
+
+
+FIELDS = KCONV + 6
+
+
+def finish_kernel(rows_in, rows_out, *refs):
+    (tokens, cotangent, norm_gain, grad_proj, gate_low, in_full, out_full) = refs[:7]
+    (sum_conv, sum_gate, sum_head) = refs[7:10]
+    (block_out, input_grad, inward, outward) = refs[10:14]
+    (norm_grad, kernel_grad, offset_grad, gain_grad, step_grad, decay_grad, skip_grad) = refs[14:21]
+    refs = refs[21:]
+    (normed_t, small_out, norm_sum) = refs[:3]
+    refs = refs[3:]
+    place = Place()
+    cuts = (grad_proj.shape[1] // (2 * LANES) * LANES, tokens.shape[1] // 2, FIELDS * LANES // 2)
+    reduce_in, reduce_out, reduce_small = [
+        Reduce(place, refs[11 * k : 11 * k + 11], cuts[k]) for k in range(3)
+    ]
+    length = tokens.shape[0]
+    width = tokens.shape[1]
+    columns = grad_proj.shape[1]
+    count = 32
+    place.greet()
+
+    gain = norm_gain[...]
+
+    def normalize(c, carry):
+        rows = pl.ds(pl.multiple_of(c * Q, Q), Q)
+        values = tokens[rows, :].astype(f32)
+        scale = lax.rsqrt(jnp.sum(values * values, axis=1, keepdims=True) * (1.0 / width) + epsilon)
+        normed_t[c] = (values * scale * gain).T.astype(bf16)
+        return carry
+
+    lax.fori_loop(0, length // Q, normalize, 0)
+
+    def multiply_in(o):
+        plane = place.planes[o]
+        at = pl.multiple_of(plane * (8 * rows_in), 64)
+        left = jnp.concatenate(
+            [normed_t[c, pl.ds(at, 8 * rows_in), :] for c in range(length // Q)], axis=1
+        )
+        for lane in range(0, columns, 512):
+            size = min(512, columns - lane)
+            block = mm(left, grad_proj[:, pl.ds(lane, size)])
+            for k in range(8):
+                reduce_in.part[plane, k // 4, (k // 2) % 2, k % 2, :, pl.ds(lane, size)] = block[
+                    k * rows_in : (k + 1) * rows_in, :
+                ].astype(bf16)
+        reduce_in.give(o)
+
+    def multiply_out(o):
+        plane = place.planes[o]
+        at = pl.multiple_of(plane * (8 * rows_out), LANES)
+        left = gate_low[:, pl.ds(at, 8 * rows_out)].astype(f32).T.astype(bf16)
+        block = mm(left, cotangent[...])
+        for k in range(8):
+            reduce_out.part[plane, k // 4, (k // 2) % 2, k % 2] = block[
+                k * rows_out : (k + 1) * rows_out, :
+            ].astype(bf16)
+        reduce_out.give(o)
+
+    norm_sum[...] = jnp.zeros_like(norm_sum)
+
+    def inputs_of(c):
+        rows = pl.ds(pl.multiple_of(c * Q, Q), Q)
+        values = tokens[rows, :].astype(f32)
+        grad_normed = mm_nt(grad_proj[rows, :], in_full[...])
+        scale = lax.rsqrt(jnp.sum(values * values, axis=1, keepdims=True) * (1.0 / width) + epsilon)
+        norm_sum[...] += fold_rows(grad_normed * (values * scale))
+        weighted = grad_normed * gain
+        mean = jnp.sum(weighted * values, axis=1, keepdims=True) * (1.0 / width)
+        back = scale * weighted - values * (scale * scale * scale * mean)
+        input_grad[rows, :] = (back + cotangent[rows, :].astype(f32)).astype(bf16)
+        block_out[rows, :] = (values + mm(gate_low[rows, :], out_full[...])).astype(bf16)
+
+
+    def total_of(ref, k):
+        return jnp.sum(ref[8 * k : 8 * k + 8, :], axis=0, keepdims=True)
+
+    part_small = reduce_small.part
+
+    def spread_slots(row, field, per):
+        for r in range(count):
+            part_small[r // 8, (r // 4) % 2, (r // 2) % 2, r % 2, :, pl.ds(field * LANES, per)] = row[:, r * per : (r + 1) * per]
+
+    def small_parts():
+
+        part_small[...] = jnp.zeros_like(part_small)
+        spread_slots(total_of(norm_sum, 0), 0, width // count)
+        for k in range(KCONV + 1):
+            spread_slots(total_of(sum_conv, k), 1 + k, DC // count)
+        spread_slots(total_of(sum_gate, 0), 2 + KCONV, DI // count)
+        skip_row = jnp.broadcast_to(total_of(sum_gate, 1), (8, DI))
+        lane_head = lax.broadcasted_iota(jnp.int32, (DI, NHEADS), 0) // HEADDIM
+        pick = (lane_head == lax.broadcasted_iota(jnp.int32, (DI, NHEADS), 1)).astype(f32)
+        per_head = [
+            total_of(sum_head, 0)[:, :NHEADS],
+            total_of(sum_head, 1)[:, :NHEADS],
+            mm_exact(skip_row, pick)[0:1, :],
+        ]
+        for k in range(3):
+            for r in range(count):
+                part_small[
+                    r // 8, (r // 4) % 2, (r // 2) % 2, r % 2, :, pl.ds((3 + KCONV + k) * LANES, NHEADS)
+                ] = per_head[k]
+
+        for o in around:
+            reduce_small.give(o)
+
+    around = (3, 2, 1, 0)
+    units = [(reduce_in, multiply_in, o) for o in around]
+    units += [(reduce_out, multiply_out, o) for o in around]
+    units += [(reduce_small, None, o) for o in around]
+    totals = {}
+
+    def advance(k, stage):
+        if 0 <= k < len(units):
+            reduce, multiply, o = units[k]
+            if stage == 0 and multiply:
+                multiply(o)
+            if stage == 1:
+                reduce.cores(o)
+            if stage == 2:
+                reduce.firsts(o)
+            if stage == 3:
+                totals[reduce] = reduce.seconds(o)
+
+    for k in range(len(units) + 5):
+        advance(k, 0)
+        advance(k - 1, 1)
+        advance(k - 3, 2)
+        advance(k - 5, 3)
+        if 3 <= k < 3 + length // Q:
+            inputs_of(k - 3)
+        if k == 3 + length // Q:
+            small_parts()
+    reduce_in.last(totals[reduce_in], inward)
+    reduce_out.last(totals[reduce_out], outward)
+    reduce_small.last(totals[reduce_small], small_out)
+
+    def field(k, size):
+        return small_out[:, pl.ds(k * LANES, size)]
+
+    norm_grad[...] = field(0, width // count)
+    for k in range(KCONV):
+        kernel_grad[k : k + 1, :] = field(1 + k, DC // count)
+    offset_grad[...] = field(1 + KCONV, DC // count)
+    gain_grad[...] = field(2 + KCONV, DI // count)
+    step_grad[...] = field(3 + KCONV, NHEADS)
+    decay_grad[...] = field(4 + KCONV, NHEADS)
+    skip_grad[...] = field(5 + KCONV, NHEADS)
+    for reduce in (reduce_in, reduce_small, reduce_out):
+        reduce.drain()
+
+
+def finish_call(tokens, cotangent, norm_gain, grad_proj, gate_low, in_full, out_full, *sums):
+    count = 32
+    length, width = tokens.shape
+    columns = grad_proj.shape[1]
+    rows_in, rows_out = width // count, DI // count
+    shape = jax.ShapeDtypeStruct
+    space = pl.BlockSpec(memory_space=pltpu.VMEM)
+    return pl.pallas_call(
+        functools.partial(finish_kernel, rows_in, rows_out),
+        name="finish",
+        out_shape=(
+            shape((length, width), bf16),
+            shape((length, width), bf16),
+            shape((rows_in, columns), f32),
+            shape((rows_out, width), f32),
+            shape((1, rows_in), f32),
+            shape((KCONV, DC // count), f32),
+            shape((1, DC // count), f32),
+            shape((1, rows_out), f32),
+            shape((1, NHEADS), f32),
+            shape((1, NHEADS), f32),
+            shape((1, NHEADS), f32),
+        ),
+        in_specs=[space] * 10,
+        out_specs=[space] * 11,
+        scratch_shapes=[
+            pltpu.VMEM((length // Q, width, Q), bf16),
+            pltpu.VMEM((1, FIELDS * LANES), f32),
+            pltpu.VMEM((8, width), f32),
+        ]
+        + Reduce.scratch(rows_in, columns, columns // (2 * LANES) * LANES, bf16)
+        + Reduce.scratch(rows_out, width, width // 2, bf16)
+        + Reduce.scratch(1, FIELDS * LANES, FIELDS * LANES // 2, f32),
+        compiler_params=pltpu.CompilerParams(
+            collective_id=4, has_side_effects=True, vmem_limit_bytes=62 * 1024 * 1024
+        ),
+    )(tokens, cotangent, norm_gain, grad_proj, gate_low, in_full, out_full, *sums)
+
+
 def rms_scale(values, weight):
     return values * lax.rsqrt(jnp.mean(values * values, axis=-1, keepdims=True) + epsilon) * weight
 
@@ -930,9 +1441,13 @@
     axes = ("dp", "seq")
     sizes = [norm_gain.shape[0], conv_weight.size, conv_bias.shape[0], gate_gain.shape[0]]
     packed = jnp.concatenate([norm_gain, conv_weight.reshape(-1), conv_bias, gate_gain])
-    in_full, out_full, packed = gather_call(
-        {"dp": dp_size, "seq": seq_size}, in_weight, out_weight, packed[None].astype(f32)
-    )
+    quick = dp_size == 4 and seq_size == 8 and in_weight.shape[0] % 8 == 0
+    quick = quick and out_weight.shape[0] % 8 == 0
+    shards = (in_weight, out_weight, packed[None].astype(f32))
+    if quick:
+        in_full, out_full, packed = quick_gather_call(*shards)
+    else:
+        in_full, out_full, packed = gather_call({"dp": dp_size, "seq": seq_size}, *shards)
     in_full = in_full.reshape(-1, in_weight.shape[1])
     out_full = out_full.reshape(-1, out_weight.shape[1])
     packed = packed[:, 0]
@@ -956,6 +1471,36 @@
     gate_low, grad_proj, sum_conv, sum_gate, sum_head = ssd_call(
         seq_size, proj, grad_low, taps_full, cbias_full, heads, gain_full
     )
+    sizes = {"dp": dp_size, "seq": seq_size}
+    count = dp_size * seq_size
+    if quick:
+        results = finish_call(
+            tokens,
+            cotangent,
+            norm_full[None],
+            grad_proj,
+            gate_low,
+            in_full,
+            out_full,
+            sum_conv,
+            sum_gate,
+            sum_head,
+        )
+        block_out, input_grad, inward, outward = results[:4]
+        norm_grad, kernel_grad, offset_grad, gain_grad, step_grad, decay_grad, skip_grad = results[4:]
+        return (
+            block_out[None],
+            input_grad[None],
+            norm_grad[0],
+            inward,
+            kernel_grad,
+            offset_grad[0],
+            step_grad[0],
+            decay_grad[0],
+            skip_grad[0],
+            gain_grad[0],
+            outward,
+        )
     block_out = (inputs + mm(gate_low, out_full)).astype(bf16)
     outward = lax.dot_general(
         gate_low, cotangent, (((0,), (0,)), ((), ())), preferred_element_type=f32
@@ -971,7 +1516,6 @@
     gate_local = jnp.sum(sum_gate.reshape(2, 8, DI), axis=1)
     head_local = jnp.sum(sum_head.reshape(2, 8, LANES), axis=1)[:, :NHEADS]
     skip_local = jnp.sum(gate_local[1].reshape(NHEADS, HEADDIM), axis=1)
-    count = dp_size * seq_size
     shared = jnp.concatenate([head_local.reshape(-1), skip_local])
     pieces = [
         norm_local.reshape(count, -1),
@@ -984,7 +1528,7 @@
     width = -(-sum(widths) // LANES) * LANES
     pieces.append(jnp.zeros((count, width - sum(widths)), f32))
     inward, outward, small = scatter_call(
-        {"dp": dp_size, "seq": seq_size},
+        sizes,
         (4, 2, 1),
         inward.astype(bf16).reshape(count, -1, inward.shape[1]),
         outward.astype(bf16).reshape(count, -1, outward.shape[1]),

time: 254 us -> 204 us (0.80)
  matrix products: 32.4 us -> 9.63 us
  Pallas kernels: 188 us -> 171 us
  local copies, waits for them, and re-layouts: 23.7 us -> 17.6 us
  other arithmetic: 8.14 us -> 3.97 us
    pallas_call x2, Pallas kernels: 114 us -> 98.5 us  [the longest x1 52.7 us: finish_call(): pl.pallas_call(functools.partial(finish_kernel, rows_in, rows_out), name=...]
    dot_general x2 -> x0, matrix products: 11.5 us -> none  [the longest x1 7.26 us: local(): lax.dot_general(normed_low, grad_proj, (((0,), (0,)), ((), ())), preferre...]
    convert_element_type x1 -> x0, local copies, waits for them, and re-layouts: 7.96 us -> none  [local(): inward.astype(bf16).reshape(count, -1, inward.shape[1])]
    unnamed x23 -> x34, local copies, waits for them, and re-layouts: 2.23 us -> 10.1 us
    dot_general x2 -> x1, matrix products: 12.9 us -> 5.08 us  [mm_nt(): lax.dot_general(a, b, (((1,), (1,)), ((), ())), preferred_element_type=f32)]
    dot_general x2 -> x1, matrix products: 7.99 us -> 4.55 us  [mm(): lax.dot_general(a, b, (((1,), (0,)), ((), ())), preferred_element_type=f32)]
    broadcast_in_dim x1 -> x0, other arithmetic: 2.93 us -> none  [local(): input_grad[None]]
where the time goes in v2:
time: 204 us
  Pallas kernels  171 us (84%)
  local copies, waits for them, and re-layouts  17.6 us (9%)
  matrix products  9.63 us (5%)
  other arithmetic  3.97 us (2%)
    pallas_call x1, Pallas kernels, ssd_call(): pl.pallas_call(functools.partial(ssd_kernel, seq_size), name='ssd', out_s...  73 us
    pallas_call x1, Pallas kernels, finish_call(): pl.pallas_call(functools.partial(finish_kernel, rows_in, rows_out), name=...  52.7 us
    pallas_call x1, Pallas kernels, quick_gather_call(): pl.pallas_call(quick_gather_kernel, name='gather', out_shape=tuple((jax.S...  45.8 us
    unnamed x34, local copies, waits for them, and re-layouts  10.1 us
    dot_general x1, matrix products, mm_nt(): lax.dot_general(a, b, (((1,), (1,)), ((), ())), preferred_element_type=f32)  5.08 us
    dot_general x1, matrix products, mm(): lax.dot_general(a, b, (((1,), (0,)), ((), ())), preferred_element_type=f32)  4.55 us

profile of v2, /device:TPU:0, one launch (start us, length us, event | category | flops | bytes accessed | tf_op | source)
XLA Modules:
  0.0 203.5 jit_solution(4574591859766268092)
XLA Ops:
  0.6 0.8 concatenate.19
  1.4 1.3 maximum_convert_fusion.refs_2_
  2.7 1.3 pad_maximum_fusion.heads
  4.0 1.4 multiply_reduce_fusion
  5.4 45.8 %gather.1 = (bf16[32,24,3352]{2,1,0:T(8,128)(2,1)}, bf16[32,48,768]{2,1,0:T(8,128)(2,1)}, f32[32,1,352]{2,1,0:T(1,128)}) custom-call(bf16[24,3352]{1,0:T(8,128)(2,1)} %refs_0_.1, bf16[48,768]{1,0:T(8,128)(2,1)} %refs_1_.1, f32[1,352]{1,0:T(1,128)} %maximum_convert_fusion.refs_2_), custom_call_target="tpu_custom_call" | custom-call | tf_op jit(solution)/shard_map/gather/pallas_call | solution.py:1087
  51.1 0.8 copy.36
  52.0 0.7 broadcast_in_dim_reshape.4.refs_2_
  52.6 0.1 mul.26
  52.7 0.1 slice.19
  52.8 0.7 reshape.126.gain
  53.5 0.1 slice.18
  53.5 0.1 slice.17
  53.6 0.7 reshape.125.cbias
  54.3 0.1 reshape.123
  54.4 0.7 reshape.124.taps
  55.1 5.1 %convolution_bitcast_fusion.grad_low = f32[512,1536]{1,0:T(8,128)} fusion(bf16[1536,768]{1,0:T(8,128)(2,1)} %bitcast.37, bf16[1,512,768]{2,1,0:T(8,128)(2,1)} %param.12), kind=kOutput, calls=%fused_computation.1 | convolution fusion | flops 1207959552 | bytes 6291456 | tf_op jit(solution)/shard_map/dot_general | solution.py:32
  60.2 0.0 copy-done
  60.2 0.0 copy-done.1
  60.2 4.6 %convolution_convert_fusion = bf16[512,3352]{0,1:T(8,128)(2,1)S(1)} fusion(bf16[768,3352]{1,0:T(8,128)(2,1)S(1)} %bitcast.35, bf16[1,512,768]{2,1,0:T(8,128)(2,1)S(1)} %copy-done.1, f32[768]{0:T(1024)S(1)} %mul.26, f32[512]{0:T(512)S(1)} %add_rsqrt_fusion), kind=kOutput, calls=%fused_computation | convolution fusion | flops 2639409152 | bytes 9372672 | tf_op jit(solution)/shard_map/dot_general | solution.py:28
  64.8 3.6 %copy.30.proj = bf16[512,3352]{1,0:T(8,128)(2,1)} copy(bf16[512,3352]{0,1:T(8,128)(2,1)S(1)} %convolution_convert_fusion) | data formatting | bytes 6864896 | tf_op jit(solution)/shard_map/convert_element_type | solution.py:1469
  68.4 73.0 %ssd.1 = (bf16[512,1536]{1,0:T(8,128)(2,1)}, bf16[512,3352]{1,0:T(8,128)(2,1)}, f32[40,1792]{1,0:T(8,128)}, f32[16,1536]{1,0:T(8,128)}, f32[16,128]{1,0:T(8,128)}) custom-call(bf16[512,3352]{1,0:T(8,128)(2,1)} %copy.30.proj, f32[512,1536]{1,0:T(8,128)} %convolution_bitcast_fusion.grad_low, f32[4,1792]{1,0:T(4,128)} %reshape.124.taps, ...), custom_call_target="tpu_custom_call" | custom-call | tf_op jit(solution)/shard_map/ssd/pallas_call | solution.py:585
  141.4 52.7 %finish.1 = (bf16[512,768]{1,0:T(8,128)(2,1)}, bf16[512,768]{1,0:T(8,128)(2,1)}, f32[24,3352]{1,0:T(8,128)}, f32[48,768]{1,0:T(8,128)}, f32[1,24]{1,0:T(1,128)},...) custom-call(bf16[512,768]{1,0:T(8,128)(2,1)} %bitcast.36, ...), custom_call_target="tpu_custom_call" | custom-call | tf_op jit(solution)/shard_map/finish/pallas_call | solution.py:1390
  194.2 0.0 copy-start.10
  194.2 0.0 copy-start.2
  194.2 0.0 copy-start.4
  194.2 0.0 copy-start.9
  194.2 0.0 copy-start.8
  194.2 0.0 copy-start.7
  194.2 0.0 copy-start.6
  194.2 0.0 copy-start.5
  194.2 0.0 copy-start.3
  194.3 2.1 %copy.48 = bf16[1,512,768]{2,1,0:T(8,128)(2,1)} copy(bf16[1,512,768]{2,1,0:T(8,128)(2,1)} %bitcast.40) | data formatting | bytes 1572864
  196.4 2.1 %copy.49 = bf16[1,512,768]{2,1,0:T(8,128)(2,1)} copy(bf16[1,512,768]{2,1,0:T(8,128)(2,1)} %bitcast.39) | data formatting | bytes 1572864
  198.4 0.0 copy-done.10
  198.5 0.5 copy.50
  199.0 0.0 copy-done.2
  199.0 0.7 copy.51
  199.7 0.0 copy-done.4
  199.7 0.6 copy.52
  200.3 0.0 copy-done.9
  200.3 0.5 copy.53
  200.8 0.5 copy.54
  201.3 0.0 copy-done.7
  201.3 0.5 copy.55
  201.8 0.0 copy-done.6
  201.8 0.5 copy.56
  202.3 0.5 copy.57
  202.9 0.7 copy.58
  (8 shorter events, 0.0 us)
Async XLA Ops:
  55.1 5.1 %copy-start = (bf16[32,24,3352]{2,1,0:T(8,128)(2,1)S(1)}, bf16[32,24,3352]{2,1,0:T(8,128)(2,1)}, u32[]{:S(2)}) copy-start(bf16[32,24,3352]{2,1,0:T(8,128)(2,1)} %get-tuple-element.31) | copy-start | bytes 15446020
  55.1 5.1 %copy-start.1 = (bf16[1,512,768]{2,1,0:T(8,128)(2,1)S(1)}, bf16[1,512,768]{2,1,0:T(8,128)(2,1)}, u32[]{:S(2)}) copy-start(bf16[1,512,768]{2,1,0:T(8,128)(2,1)} %param.11) | copy-start | bytes 2359300
  194.2 4.3 %copy-start.10 = (f32[1,24]{1,0:T(1,128)S(1)}, f32[1,24]{1,0:T(1,128)}, u32[]{:S(2)}) copy-start(f32[1,24]{1,0:T(1,128)} %get-tuple-element.40) | copy-start | bytes 292
  194.2 4.8 %copy-start.2 = (f32[24,3352]{1,0:T(8,128)S(1)}, f32[24,3352]{1,0:T(8,128)}, u32[]{:S(2)}) copy-start(f32[24,3352]{1,0:T(8,128)} %get-tuple-element.63) | copy-start | bytes 965380
  194.2 5.5 %copy-start.4 = (f32[4,56]{1,0:T(4,128)S(1)}, f32[4,56]{1,0:T(4,128)}, u32[]{:S(2)}) copy-start(f32[4,56]{1,0:T(4,128)} %get-tuple-element.64) | copy-start | bytes 2692
  194.2 6.1 %copy-start.9 = (f32[1,56]{1,0:T(1,128)S(1)}, f32[1,56]{1,0:T(1,128)}, u32[]{:S(2)}) copy-start(f32[1,56]{1,0:T(1,128)} %get-tuple-element.43) | copy-start | bytes 676
  194.2 6.6 %copy-start.8 = (f32[1,24]{1,0:T(1,128)S(1)}, f32[1,24]{1,0:T(1,128)}, u32[]{:S(2)}) copy-start(f32[1,24]{1,0:T(1,128)} %get-tuple-element.44) | copy-start | bytes 292
  194.2 7.1 %copy-start.7 = (f32[1,24]{1,0:T(1,128)S(1)}, f32[1,24]{1,0:T(1,128)}, u32[]{:S(2)}) copy-start(f32[1,24]{1,0:T(1,128)} %get-tuple-element.45) | copy-start | bytes 292
  194.2 7.6 %copy-start.6 = (f32[1,24]{1,0:T(1,128)S(1)}, f32[1,24]{1,0:T(1,128)}, u32[]{:S(2)}) copy-start(f32[1,24]{1,0:T(1,128)} %get-tuple-element.46) | copy-start | bytes 292
  194.2 8.1 %copy-start.5 = (f32[1,48]{1,0:T(1,128)S(1)}, f32[1,48]{1,0:T(1,128)}, u32[]{:S(2)}) copy-start(f32[1,48]{1,0:T(1,128)} %get-tuple-element.47) | copy-start | bytes 580
  194.2 8.6 %copy-start.3 = (f32[48,768]{1,0:T(8,128)S(1)}, f32[48,768]{1,0:T(8,128)}, u32[]{:S(2)}) copy-start(f32[48,768]{1,0:T(8,128)} %get-tuple-element.70) | copy-start | bytes 442372
